TPU v7x, 32 devices: a whole 2x2x4 slice. The times are simulated.
32 devices in a mesh: shard: 8 (over y, x, core), tensor: 4 (over z).
Axes of the slice: x: 2, y: 2, z: 4, core: 2. Of those that a mesh axis runs over, the one named last changes fastest.
Arguments:
- tokens: bfloat16 [16384, 2048], P('shard'), may hold values from -40 to 40
- ln1_gain: bfloat16 [2048], P('shard'), may hold values from 0.25 to 1.75
- ln1_bias: bfloat16 [2048], P('shard'), may hold values from -3 to 3
- qkv_weight: bfloat16 [2048, 8, 3, 256], P('shard', 'tensor'), may hold values from -2 to 2
- qkv_bias: bfloat16 [8, 3, 256], P('tensor'), may hold values from -3 to 3
- out_weight: bfloat16 [2048, 8, 256], P('shard', 'tensor'), may hold values from -0.5 to 0.5
- out_bias: bfloat16 [2048], P('shard'), may hold values from -3 to 3
- ln2_gain: bfloat16 [2048], P('shard'), may hold values from 0.25 to 1.75
- ln2_bias: bfloat16 [2048], P('shard'), may hold values from -3 to 3
- fc1_weight: bfloat16 [2048, 8192], P('shard', 'tensor'), may hold values from -0.125 to 0.125
- fc1_bias: bfloat16 [8192], P('tensor'), may hold values from -3 to 3
- fc2_weight: bfloat16 [2048, 8192], P('shard', 'tensor'), may hold values from -0.0625 to 0.0625
- fc2_bias: bfloat16 [2048], P('shard'), may hold values from -3 to 3
- cotangent: bfloat16 [16384, 2048], P('shard'), may hold values from -6 to 6
Outputs:
- block_out: bfloat16 [16384, 2048], P('shard')
- grad_tokens: float32 [16384, 2048], P('shard')
- grad_ln1_gain: float32 [2048], P('shard')
- grad_ln1_bias: float32 [2048], P('shard')
- grad_qkv_weight: float32 [2048, 8, 3, 256], P('shard', 'tensor')
- grad_qkv_bias: float32 [8, 3, 256], P('tensor')
- grad_out_weight: float32 [2048, 8, 256], P('shard', 'tensor')
- grad_out_bias: float32 [2048], P('shard')
- grad_ln2_gain: float32 [2048], P('shard')
- grad_ln2_bias: float32 [2048], P('shard')
- grad_fc1_weight: float32 [2048, 8192], P('shard', 'tensor')
- grad_fc1_bias: float32 [8192], P('tensor')
- grad_fc2_weight: float32 [2048, 8192], P('shard', 'tensor')
- grad_fc2_bias: float32 [2048], P('shard')
All inputs are finite; a program needn't handle non-finite values.
Results may differ from a plain program's by a relative error of at most 0.017.
Values may be sent and summed in bfloat16 or wider, within the bound.
A program may use at most 320 MiB of HBM per device.

v0:
```python
import math

import jax
import jax.numpy as jnp
from jax import lax
from jax.sharding import PartitionSpec as P

ROT = 64
SEQ = 256
MICRO = 2


NORM_EPS = 1e-05
ROOT_HALF = 0.7071067811865476
INV_ROOT_TWO_PI = 0.3989422804014327


def as_sent(shard):

    def short(part):
        return part.astype(jnp.bfloat16) if part.dtype == jnp.float32 else part

    return jax.tree.map(short, shard)


def normalize(residual):
    row_mean = jnp.mean(residual, axis=-1, keepdims=True)
    centered = residual - row_mean
    row_var = jnp.mean(centered * centered, axis=-1, keepdims=True)
    inv_std = lax.rsqrt(row_var + NORM_EPS)
    return (centered * inv_std, inv_std)


def norm_backward(grad_normed, gain_wide, normalized, inv_std):
    scaled_grad = grad_normed * gain_wide
    return inv_std * (
        scaled_grad
        - jnp.mean(scaled_grad, axis=-1, keepdims=True)
        - normalized * jnp.mean(scaled_grad * normalized, axis=-1, keepdims=True)
    )


def rotary_tables(length, rot_dims):
    half_dims = rot_dims // 2
    frequency = jnp.power(10000.0, -2.0 * jnp.arange(half_dims, dtype=jnp.float32) / rot_dims)
    angles = jnp.arange(length, dtype=jnp.float32)[:, None] * frequency[None, :]
    return (jnp.cos(angles), jnp.sin(angles))


def rotate(field, cos_tab, sin_tab, rot_dims):
    half_dims = rot_dims // 2
    lower_half = field[..., :half_dims]
    upper_half = field[..., half_dims:rot_dims]
    cos_wide = cos_tab[None, :, None, :]
    sin_wide = sin_tab[None, :, None, :]
    return jnp.concatenate(
        [
            lower_half * cos_wide - upper_half * sin_wide,
            upper_half * cos_wide + lower_half * sin_wide,
            field[..., rot_dims:],
        ],
        axis=-1,
    )


def rotate_back(grad_field, cos_tab, sin_tab, rot_dims):
    half_dims = rot_dims // 2
    lower_half = grad_field[..., :half_dims]
    upper_half = grad_field[..., half_dims:rot_dims]
    cos_wide = cos_tab[None, :, None, :]
    sin_wide = sin_tab[None, :, None, :]
    return jnp.concatenate(
        [
            lower_half * cos_wide + upper_half * sin_wide,
            upper_half * cos_wide - lower_half * sin_wide,
            grad_field[..., rot_dims:],
        ],
        axis=-1,
    )


def gelu_exact(pre_act):
    return 0.5 * pre_act * (1.0 + lax.erf(pre_act * ROOT_HALF))


def gelu_slope(pre_act):
    return (
        0.5 * (1.0 + lax.erf(pre_act * ROOT_HALF))
        + pre_act * jnp.exp(-0.5 * pre_act * pre_act) * INV_ROOT_TWO_PI
    )


def causal_scores(queries, key_rows, score_scale):
    length = queries.shape[1]
    scores = (
        jnp.einsum("nqhc,nkhc->nhqk", queries, key_rows, preferred_element_type=jnp.float32)
        * score_scale
    )
    causal = jnp.arange(length)[:, None] >= jnp.arange(length)[None, :]
    return jnp.where(causal[None, None], scores, -1e30)


def add_pairs(older, newer):
    return tuple((first_term + second_term for first_term, second_term in zip(older, newer)))


def forward_pass(x_block, weights, qkv_shift, fc1_shift, cos_tab, sin_tab):
    (
        qkv_full,
        out_full,
        fc1_full,
        fc2_full,
        gain_one,
        bias_one,
        gain_two,
        bias_two,
        out_shift,
        fc2_shift,
    ) = weights
    row_count = x_block.shape[0]
    seq_count = row_count // SEQ
    head_count = qkv_full.shape[1]
    head_dim = qkv_full.shape[3]
    residual = x_block.astype(jnp.float32)
    normalized, inv_std = normalize(residual)
    normed_one = (normalized * gain_one.astype(jnp.float32) + bias_one.astype(jnp.float32)).astype(
        jnp.bfloat16
    )
    normed_two = (normalized * gain_two.astype(jnp.float32) + bias_two.astype(jnp.float32)).astype(
        jnp.bfloat16
    )
    qkv = jnp.einsum("md,dhkc->mhkc", normed_one, qkv_full, preferred_element_type=jnp.float32)
    qkv = qkv + qkv_shift.astype(jnp.float32)
    fields = qkv.reshape(seq_count, SEQ, head_count, 3, head_dim)
    queries = rotate(fields[:, :, :, 0], cos_tab, sin_tab, ROT).astype(jnp.bfloat16)
    key_rows = rotate(fields[:, :, :, 1], cos_tab, sin_tab, ROT).astype(jnp.bfloat16)
    values = fields[:, :, :, 2].astype(jnp.bfloat16)
    score_scale = 1.0 / math.sqrt(head_dim)
    scores = causal_scores(queries, key_rows, score_scale)
    row_top = jnp.max(scores, axis=-1, keepdims=True)
    log_total = row_top + jnp.log(jnp.sum(jnp.exp(scores - row_top), axis=-1, keepdims=True))
    attn_probs = jnp.exp(scores - log_total).astype(jnp.bfloat16)
    attn_out = jnp.einsum("nhqk,nkhc->nqhc", attn_probs, values, preferred_element_type=jnp.float32)
    attn_out = attn_out.astype(jnp.bfloat16).reshape(row_count, head_count, head_dim)
    pre_act = jnp.dot(normed_two, fc1_full, preferred_element_type=jnp.float32) + fc1_shift.astype(
        jnp.float32
    )
    hidden = gelu_exact(pre_act).astype(jnp.bfloat16)
    partial_value = jnp.einsum(
        "mhc,dhc->md", attn_out, out_full, preferred_element_type=jnp.float32
    )
    partial_value = partial_value + jnp.einsum(
        "mf,df->md", hidden, fc2_full, preferred_element_type=jnp.float32
    )
    saved = (
        residual,
        normalized,
        inv_std,
        normed_one,
        normed_two,
        queries,
        key_rows,
        values,
        log_total,
        attn_out,
        pre_act,
        hidden,
    )
    return (partial_value, saved)


def backward_pass(grad_block, saved, weights, cos_tab, sin_tab):
    (
        qkv_full,
        out_full,
        fc1_full,
        fc2_full,
        gain_one,
        bias_one,
        gain_two,
        bias_two,
        out_shift,
        fc2_shift,
    ) = weights
    (
        residual,
        normalized,
        inv_std,
        normed_one,
        normed_two,
        queries,
        key_rows,
        values,
        log_total,
        attn_out,
        pre_act,
        hidden,
    ) = saved
    row_count = grad_block.shape[0]
    seq_count = row_count // SEQ
    head_count = qkv_full.shape[1]
    head_dim = qkv_full.shape[3]
    score_scale = 1.0 / math.sqrt(head_dim)
    grad_wide = grad_block.astype(jnp.float32)
    shift_grad = jnp.sum(grad_wide, axis=0)
    grad_out_w = jnp.einsum("md,mhc->dhc", grad_block, attn_out, preferred_element_type=jnp.float32)
    grad_fc2_w = jnp.einsum("md,mf->df", grad_block, hidden, preferred_element_type=jnp.float32)
    d_attn = jnp.einsum("md,dhc->mhc", grad_block, out_full, preferred_element_type=jnp.float32)
    d_attn = d_attn.astype(jnp.bfloat16).reshape(seq_count, SEQ, head_count, head_dim)
    d_pre = jnp.dot(grad_block, fc2_full, preferred_element_type=jnp.float32) * gelu_slope(pre_act)
    fc1_shift_grad = jnp.sum(d_pre, axis=0)
    d_pre_b = d_pre.astype(jnp.bfloat16)
    grad_fc1_w = jnp.einsum("md,mf->df", normed_two, d_pre_b, preferred_element_type=jnp.float32)
    d_two = jnp.einsum("mf,df->md", d_pre_b, fc1_full, preferred_element_type=jnp.float32)
    probs_again = jnp.exp(causal_scores(queries, key_rows, score_scale) - log_total)
    d_values = jnp.einsum(
        "nhqk,nqhc->nkhc",
        probs_again.astype(jnp.bfloat16),
        d_attn,
        preferred_element_type=jnp.float32,
    )
    d_probs = jnp.einsum("nqhc,nkhc->nhqk", d_attn, values, preferred_element_type=jnp.float32)
    row_delta = jnp.sum(probs_again * d_probs, axis=-1, keepdims=True)
    d_scores = (probs_again * (d_probs - row_delta) * score_scale).astype(jnp.bfloat16)
    d_queries = rotate_back(
        jnp.einsum("nhqk,nkhc->nqhc", d_scores, key_rows, preferred_element_type=jnp.float32),
        cos_tab,
        sin_tab,
        ROT,
    )
    d_keys = rotate_back(
        jnp.einsum("nhqk,nqhc->nkhc", d_scores, queries, preferred_element_type=jnp.float32),
        cos_tab,
        sin_tab,
        ROT,
    )
    d_qkv = jnp.stack([d_queries, d_keys, d_values], axis=3).reshape(
        row_count, head_count, 3, head_dim
    )
    qkv_shift_grad = jnp.sum(d_qkv, axis=0)
    d_qkv_b = d_qkv.astype(jnp.bfloat16)
    grad_qkv_w = jnp.einsum(
        "md,mhkc->dhkc", normed_one, d_qkv_b, preferred_element_type=jnp.float32
    )
    d_one = jnp.einsum("mhkc,dhkc->md", d_qkv_b, qkv_full, preferred_element_type=jnp.float32)
    d_input = norm_backward(
        d_one, gain_one.astype(jnp.float32), normalized, inv_std
    ) + norm_backward(d_two, gain_two.astype(jnp.float32), normalized, inv_std)
    norm_terms = jnp.stack(
        [
            jnp.sum(d_one * normalized, axis=0),
            jnp.sum(d_one, axis=0),
            jnp.sum(d_two * normalized, axis=0),
            jnp.sum(d_two, axis=0),
        ]
    )
    matrix_grads = (grad_qkv_w, grad_out_w, grad_fc1_w, grad_fc2_w)
    return (d_input, norm_terms, matrix_grads, shift_grad, qkv_shift_grad, fc1_shift_grad)


def per_device(
    tokens,
    ln1_gain,
    ln1_bias,
    qkv_weight,
    qkv_bias,
    out_weight,
    out_bias,
    ln2_gain,
    ln2_bias,
    fc1_weight,
    fc1_bias,
    fc2_weight,
    fc2_bias,
    cotangent,
):
    own_shards = (
        qkv_weight,
        out_weight,
        fc1_weight,
        fc2_weight,
        ln1_gain,
        ln1_bias,
        ln2_gain,
        ln2_bias,
        out_bias,
        fc2_bias,
    )
    micro_rows = tokens.shape[0] // MICRO
    cos_tab, sin_tab = rotary_tables(SEQ, ROT)
    outputs = []
    grad_outputs = []
    grad_accum = None
    qkv_shift_acc = jnp.zeros(qkv_bias.shape, jnp.float32)
    fc1_shift_acc = jnp.zeros(fc1_bias.shape, jnp.float32)
    for micro_index in range(MICRO):
        x_block = tokens[micro_index * micro_rows : (micro_index + 1) * micro_rows]
        grad_block = cotangent[micro_index * micro_rows : (micro_index + 1) * micro_rows]
        forward_weights = (
            lax.all_gather(own_shards[0], "shard", axis=0, tiled=True),
            lax.all_gather(own_shards[1], "shard", axis=0, tiled=True),
            lax.all_gather(own_shards[2], "shard", axis=0, tiled=True),
            lax.all_gather(own_shards[3], "shard", axis=0, tiled=True),
            lax.all_gather(own_shards[4], "shard", axis=0, tiled=True),
            lax.all_gather(own_shards[5], "shard", axis=0, tiled=True),
            lax.all_gather(own_shards[6], "shard", axis=0, tiled=True),
            lax.all_gather(own_shards[7], "shard", axis=0, tiled=True),
            lax.all_gather(own_shards[8], "shard", axis=0, tiled=True),
            lax.all_gather(own_shards[9], "shard", axis=0, tiled=True),
        )
        partial_value, saved = forward_pass(
            x_block, forward_weights, qkv_bias, fc1_bias, cos_tab, sin_tab
        )
        branch_total = lax.psum(partial_value.astype(jnp.bfloat16), "tensor").astype(jnp.float32)
        shifts = forward_weights[8].astype(jnp.float32) + forward_weights[9].astype(jnp.float32)
        outputs.append((saved[0] + branch_total + shifts).astype(jnp.bfloat16))
        backward_weights = (
            lax.all_gather(own_shards[0], "shard", axis=0, tiled=True),
            lax.all_gather(own_shards[1], "shard", axis=0, tiled=True),
            lax.all_gather(own_shards[2], "shard", axis=0, tiled=True),
            lax.all_gather(own_shards[3], "shard", axis=0, tiled=True),
            lax.all_gather(own_shards[4], "shard", axis=0, tiled=True),
            lax.all_gather(own_shards[5], "shard", axis=0, tiled=True),
            lax.all_gather(own_shards[6], "shard", axis=0, tiled=True),
            lax.all_gather(own_shards[7], "shard", axis=0, tiled=True),
            lax.all_gather(own_shards[8], "shard", axis=0, tiled=True),
            lax.all_gather(own_shards[9], "shard", axis=0, tiled=True),
        )
        d_input, norm_terms, matrix_grads, shift_grad, qkv_shift_grad, fc1_shift_grad = (
            backward_pass(grad_block, saved, backward_weights, cos_tab, sin_tab)
        )
        summed_input, summed_norms = (
            lax.psum(d_input.astype(jnp.bfloat16), "tensor").astype(jnp.float32),
            lax.psum(norm_terms.astype(jnp.bfloat16), "tensor").astype(jnp.float32),
        )
        grad_outputs.append(grad_block.astype(jnp.float32) + summed_input)
        grad_terms = matrix_grads + (
            summed_norms[0],
            summed_norms[1],
            summed_norms[2],
            summed_norms[3],
            shift_grad,
        )
        grad_accum = grad_terms if micro_index == 0 else add_pairs(grad_accum, grad_terms)
        qkv_shift_acc = qkv_shift_acc + qkv_shift_grad
        fc1_shift_acc = fc1_shift_acc + fc1_shift_grad
    shares = jax.tree.map(
        lambda part: part.astype(jnp.float32),
        lax.psum_scatter(as_sent(grad_accum), "shard", scatter_dimension=0, tiled=True),
    )
    qkv_shift_sum, fc1_shift_sum = lax.psum((qkv_shift_acc, fc1_shift_acc), "shard")
    return (
        jnp.concatenate(outputs, axis=0),
        jnp.concatenate(grad_outputs, axis=0),
        shares[4],
        shares[5],
        shares[0],
        qkv_shift_sum,
        shares[1],
        shares[8],
        shares[6],
        shares[7],
        shares[2],
        fc1_shift_sum,
        shares[3],
        shares[8],
    )


def solution(mesh):
    return jax.shard_map(
        per_device,
        mesh=mesh,
        in_specs=(
            P("shard", None),
            P("shard"),
            P("shard"),
            P("shard", "tensor", None, None),
            P("tensor", None, None),
            P("shard", "tensor", None),
            P("shard"),
            P("shard"),
            P("shard"),
            P("shard", "tensor"),
            P("tensor"),
            P("shard", "tensor"),
            P("shard"),
            P("shard", None),
        ),
        out_specs=(
            P("shard", None),
            P("shard", None),
            P("shard"),
            P("shard"),
            P("shard", "tensor", None, None),
            P("tensor", None, None),
            P("shard", "tensor", None),
            P("shard"),
            P("shard"),
            P("shard"),
            P("shard", "tensor"),
            P("tensor"),
            P("shard", "tensor"),
            P("shard"),
        ),
        check_vma=False,
    )
```

profile of v0, /device:TPU:0, one launch (start us, length us, event | category | flops | bytes accessed | tf_op | source)
XLA Modules:
  0.0 1115.3 jit_solution(9230165923432377804)
XLA Ops:
  71.8 17.2 %all-gather.11.cloned.1.call-done = bf16[2048,2,3,256]{3,0,2,1:T(8,128)(2,1)} async-done(((bf16[256,2,3,256]{3,0,2,1:T(8,128)(2,1)}), bf16[2048,2,3,256]{3,0,2,1:T(8,128)(2,1)}) %all-gather.11.cloned.1.call-update) | async-done | bytes 6291472 | tf_op jit(solution)/shard_map/all_gather | solution.py:300
  89.0 11.2 %broadcast_add_fusion = f32[1024,2,3,256]{3,0,2,1:T(8,128)S(1)} fusion(f32[2,3,256]{2,1,0:T(4,128)S(1)} %copy.111, bf16[2048,2,3,256]{3,0,2,1:T(8,128)(2,1)} %all-gather.11.cloned.1.call-done, f32[1024]{0:T(1024)S(1)} %add_rsqrt_fusion, f32[1024]{0:T(1024)S(1)} %get-tuple-element.149, f32[2048]{0:T(1024)S(1)} %bitcast.255, f32[2048]{0:T(1024)S(1)} %bitcast.239, ...), kind=kOutput, calls=%fused_computation.115 | convolution fusion | flops 6456606720 | bytes 16807936 | tf_op jit(solution)/shard_map/md,dhkc->mhkc/dot_general | solution.py:132
  177.8 14.8 %fusion.146 = f32[2048,2,3,256]{3,0,2,1:T(8,128)} fusion(f32[2048]{0:T(1024)S(1)} %bitcast.257, f32[2048]{0:T(1024)S(1)} %bitcast.241, f32[1024]{0:T(1024)S(1)} %add_rsqrt_fusion.1, f32[1024]{0:T(1024)S(1)} %get-tuple-element.150, f32[1024,2,1,256]{3,0,2,1:T(8,128)} %bitcast.198, f32[1024,2,1,256]{3,0,2,1:T(8,128)} %bitcast.201, ...), kind=kOutput, calls=%fused_computation.178 | convolution fusion | flops 6464471040 | bytes 23093248 | tf_op jit(solution)/shard_map/md,mhkc->dhkc/dot_general | solution.py:242
  205.5 15.2 %add_convert_fusion.2 = bf16[2048,2,3,256]{3,0,2,1:T(8,128)(2,1)} fusion(f32[2048,2,3,256]{3,0,2,1:T(8,128)} %fusion.146, f32[1024]{0:T(1024)S(1)} %add_rsqrt_fusion, f32[1024]{0:T(1024)S(1)} %get-tuple-element.149, f32[2048]{0:T(1024)S(1)} %bitcast.258, f32[2048]{0:T(1024)S(1)} %bitcast.242, f32[1024,2,1,256]{3,0,2,1:T(8,128)S(1)} %bitcast.207, ...), kind=kOutput, calls=%fused_computation.5 | convolution fusion | flops 6470762496 | bytes 29384704 | tf_op jit(solution)/shard_map/md,mhkc->dhkc/dot_general | solution.py:242
  221.5 12.8 %fusion.209 = f32[1024,2048]{1,0:T(8,128)S(1)} fusion(bf16[2048,2048]{1,0:T(8,128)(2,1)} %all-gather.15.cloned.1.call-done, f32[1024]{0:T(1024)S(1)} %add_rsqrt_fusion, f32[1024]{0:T(1024)S(1)} %get-tuple-element.149, f32[2048]{0:T(1024)S(1)} %bitcast.251, f32[2048]{0:T(1024)S(1)} %bitcast.232, bf16[2048,2048]{1,0:T(8,128)(2,1)} %param.14), kind=kOutput, calls=%fused_computation.270 | convolution fusion | flops 8602517504 | bytes 20996096 | tf_op jit(solution)/shard_map/dot_general | solution.py:145
  237.5 15.7 %multiply_convert_fusion.1 = (bf16[1024,2048]{1,0:T(8,128)(2,1)}, bf16[1024,2048]{1,0:T(8,128)(2,1)}, f32[1024,2048]{1,0:T(8,128)}) fusion(f32[2048]{0:T(1024)S(1)} %copy-done.43, f32[1024,2048]{1,0:T(8,128)S(1)} %fusion.209, bf16[2048,2048]{1,0:T(8,128)(2,1)S(1)} %copy-done.49, f32[2048]{0:T(1024)S(1)} %bitcast.252, f32[2048]{0:T(1024)S(1)} %bitcast.233, ...), kind=kOutput, calls=%fused_computation.92 | convolution fusion | flops 8627683328 | bytes 37781504 | tf_op jit(solution)/shard_map/dot_general | solution.py:145
  253.1 18.4 %fusion.215 = (f32[2048]{0:T(1024)}, bf16[1024,2048]{1,0:T(8,128)(2,1)S(1)}) fusion(f32[1024,2048]{1,0:T(8,128)} %get-tuple-element.139, f32[2048]{0:T(1024)S(1)} %copy-done.43, bf16[2048,2048]{1,0:T(8,128)(2,1)} %all-gather.17.cloned.1.call-done, bf16[2048,2048]{1,0:T(8,128)(2,1)} %param.27), kind=kOutput, calls=%fused_computation.275 | convolution fusion | flops 8615098368 | bytes 25182208 | tf_op jit(solution)/shard_map/dot_general | solution.py:210
  271.5 16.8 %fusion.92 = f32[2048,2048]{1,0:T(8,128)} fusion(bf16[1024,2048]{1,0:T(8,128)(2,1)S(1)} %get-tuple-element.146, f32[2048]{0:T(1024)S(1)} %bitcast.253, f32[2048]{0:T(1024)S(1)} %bitcast.234, f32[1024]{0:T(1024)S(1)} %add_rsqrt_fusion.1, f32[1024]{0:T(1024)S(1)} %get-tuple-element.150, bf16[2048,2048]{1,0:T(8,128)(2,1)} %param.14), kind=kOutput, calls=%fused_computation.138 | convolution fusion | flops 8602517504 | bytes 25190400 | tf_op jit(solution)/shard_map/md,mf->df/dot_general | solution.py:213
  288.3 16.6 %fusion.216 = (f32[2048]{0:T(1024)}, bf16[1024,2048]{1,0:T(8,128)(2,1)}) fusion(f32[1024,2048]{1,0:T(8,128)} %copy-done.59, f32[2048]{0:T(1024)S(1)} %copy-done.43, bf16[2048,2048]{1,0:T(8,128)(2,1)S(1)} %copy-done.48, bf16[2048,2048]{1,0:T(8,128)(2,1)} %param.27), kind=kOutput, calls=%fused_computation.276 | convolution fusion | flops 8615098368 | bytes 25182208 | tf_op jit(solution)/shard_map/dot_general | solution.py:210
  305.0 16.8 %add_convert_fusion.1 = bf16[2048,2048]{1,0:T(8,128)(2,1)} fusion(f32[2048,2048]{1,0:T(8,128)} %fusion.92, bf16[1024,2048]{1,0:T(8,128)(2,1)} %get-tuple-element.148, f32[1024]{0:T(1024)S(1)} %add_rsqrt_fusion, f32[1024]{0:T(1024)S(1)} %get-tuple-element.149, f32[2048]{0:T(1024)S(1)} %bitcast.254, f32[2048]{0:T(1024)S(1)} %bitcast.235, ...), kind=kOutput, calls=%fused_computation.4 | convolution fusion | flops 8610906112 | bytes 33579008 | tf_op jit(solution)/shard_map/md,mf->df/dot_general | solution.py:213
  321.9 13.6 %fusion.199 = f32[1024,2048,1,1]{1,0,3,2:T(8,128)} fusion(bf16[2048,2,3,256]{3,0,2,1:T(8,128)(2,1)} %all-gather.11.cloned.1.call-done, f32[1024,2,1,256]{3,0,2,1:T(8,128)} %bitcast.208, f32[1024,2,1,256]{3,0,2,1:T(8,128)} %bitcast.211, f32[1024,2,1,256]{3,0,2,1:T(8,128)} %bitcast.214), kind=kOutput, calls=%fused_computation.264 | convolution fusion | flops 6445596672 | bytes 20971520 | tf_op jit(solution)/shard_map/mhkc,dhkc->md/dot_general | solution.py:245
  335.5 11.4 %fusion.196 = f32[1024,2048,1,1]{1,0,3,2:T(8,128)} fusion(bf16[2048,2,3,256]{3,0,2,1:T(8,128)(2,1)} %all-gather.11.cloned.1.call-done, f32[1024,2,1,256]{3,0,2,1:T(8,128)S(1)} %bitcast.199, f32[1024,2,1,256]{3,0,2,1:T(8,128)S(1)} %bitcast.203, f32[1024,2,1,256]{3,0,2,1:T(8,128)S(1)} %bitcast.206), kind=kOutput, calls=%fused_computation.263 | convolution fusion | flops 6445596672 | bytes 20971520 | tf_op jit(solution)/shard_map/mhkc,dhkc->md/dot_general | solution.py:245
  347.0 11.7 %fusion.118 = f32[2048,2048]{1,0:T(8,128)} fusion(bf16[1024,2048]{1,0:T(8,128)(2,1)S(1)} %copy-done.60, bf16[2048,2048]{1,0:T(8,128)(2,1)S(1)} %bitcast.177), kind=kOutput, calls=%fused_computation.160 | convolution fusion | flops 8589934592 | bytes 25165824 | tf_op jit(solution)/shard_map/md,mf->df/dot_general | solution.py:207
  358.6 16.5 %fusion.64 = bf16[2048,2048]{0,1:T(8,128)(2,1)} fusion(f32[2048,2048]{1,0:T(8,128)} %fusion.118, bf16[1024,2048]{1,0:T(8,128)(2,1)} %get-tuple-element.136, bf16[2048,2048]{1,0:T(8,128)(2,1)S(1)} %bitcast.177), kind=kOutput, calls=%fused_computation.80 | convolution fusion | flops 8598323200 | bytes 33554432 | tf_op jit(solution)/shard_map/md,mf->df/dot_general | solution.py:207
  375.2 15.0 %fusion.94 = f32[1024,2048]{1,0:T(8,128)} fusion(bf16[2048,2048]{1,0:T(8,128)(2,1)} %all-gather.15.cloned.1.call-done, bf16[1024,2048]{1,0:T(8,128)(2,1)} %copy-done.62), kind=kOutput, calls=%fused_computation.140 | convolution fusion | flops 8589934592 | bytes 20971520 | tf_op jit(solution)/shard_map/mf,df->md/dot_general | solution.py:214
  390.2 30.2 %fusion.34 = (bf16[2048]{0:T(1024)(128)(2,1)S(1)}, f32[1024]{0:T(1024)S(1)}, f32[1024]{0:T(1024)S(1)}, bf16[2048]{0:T(1024)(128)(2,1)S(1)}, f32[1024]{0:T(1024)S...) fusion(f32[1024]{0:T(1024)S(1)} %add_rsqrt_fusion, ...), kind=kOutput, calls=%fused_computation.50 | convolution fusion | flops 8661213184 | bytes 54624256 | tf_op jit(solution)/shard_map/mf,df->md/dot_general | solution.py:214
  420.5 12.5 %fusion.217 = f32[1024,2048]{1,0:T(8,128)S(1)} fusion(bf16[1024,2048]{1,0:T(8,128)(2,1)S(1)} %copy-done.61, bf16[2048,2048]{1,0:T(8,128)(2,1)} %all-gather.17.cloned.1.call-done), kind=kOutput, calls=%fused_computation.277 | convolution fusion | flops 8589934592 | bytes 20971520 | tf_op jit(solution)/shard_map/mf,df->md/dot_general | solution.py:152
  437.4 14.8 %fusion.218 = f32[1024,2048]{1,0:T(8,128)} fusion(bf16[1024,2048]{1,0:T(8,128)(2,1)} %get-tuple-element.136, bf16[2048,2048]{1,0:T(8,128)(2,1)} %all-gather.17.cloned.1.call-done), kind=kOutput, calls=%fused_computation.278 | convolution fusion | flops 8589934592 | bytes 20971520 | tf_op jit(solution)/shard_map/mf,df->md/dot_general | solution.py:152
  501.3 26.1 %all-reduce.5 = (f32[2,3,256]{2,1,0:T(4,128)S(1)}, f32[2048]{0:T(1024)}) all-reduce(f32[2,3,256]{2,1,0:T(4,128)S(1)} %add.284, f32[2048]{0:T(1024)S(1)} %add.290), channel_id=1, replica_groups=mesh['shard'=8,'tensor'=4] {'shard'}, use_global_device_ids=true, to_apply=%region_37.38 | all-reduce | flops 3584 | bytes 28672 | tf_op jit(solution)/shard_map/psum | solution.py:351
  528.2 21.2 %all-reduce.7 = (bf16[4,2048]{1,0:T(4,128)(2,1)S(1)}, bf16[4,2048]{1,0:T(4,128)(2,1)S(1)}) all-reduce(bf16[4,2048]{1,0:T(4,128)(2,1)S(1)} %pad_maximum_fusion.13, bf16[4,2048]{1,0:T(4,128)(2,1)S(1)} %pad_maximum_fusion.12), channel_id=1, replica_groups=mesh['shard'=8,'tensor'=4] {'tensor'}, use_global_device_ids=true, to_apply=%region_31.32 | all-reduce | flops 16384 | bytes 65536 | tf_op jit(solution)/shard_map/psum | solution.py:334
  558.1 481.4 %all-reduce.11.cloned.1.call-done = (bf16[1024,2048]{1,0:T(8,128)(2,1)}, bf16[1024,2048]{1,0:T(8,128)(2,1)}, bf16[1024,2048]{1,0:T(8,128)(2,1)}, bf16[1024,2048]{1,0:T(8,128)(2,1)}) async-done(((bf16[1024,2048]{1,0:T(8,128)(2,1)}, bf16[1024,2048]{1,0:T(8,128)(2,1)}, bf16[1024,2048]{1,0:T(8,128)(2,1)}, bf16[1024,2048]{1,0:T(8,128)(2,1)}), (bf16[1024,2048]{1,0:T(8,128)(2,1)}, bf16[1024,2048]{1,0:T(8,128)(2,1)}, ...) | async-done | bytes 16777232 | tf_op jit(solution)/shard_map/psum | solution.py:314
  1039.5 11.3 %convert_reduce_fusion.2 = (f32[2048]{0:T(1024)S(1)}, f32[2048]{0:T(1024)S(1)}, f32[1024,2048]{1,0:T(8,128)}, f32[1024,2048]{1,0:T(8,128)}) fusion(bf16[2048,2048]{1,0:T(8,128)(2,1)} %param.27, bf16[1024,2048]{1,0:T(8,128)(2,1)} %get-tuple-element.99, bf16[1024,2048]{1,0:T(8,128)(2,1)} %get-tuple-element.100), kind=kLoop, calls=%fused_computation.14 | loop fusion | flops 16773120 | bytes 33570816 | tf_op jit(solution)/shard_map/reduce_sum | solution.py:205
  1050.8 23.8 %all-reduce.6 = (bf16[2048]{0:T(1024)(128)(2,1)S(1)}, bf16[2048]{0:T(1024)(128)(2,1)S(1)}, bf16[2048]{0:T(1024)(128)(2,1)S(1)}, bf16[2048]{0:T(1024)(128)(2,1)S(1)}, bf16[2048]{0:T(1024)(128)(2,1)S(1)}) all-reduce(bf16[2048]{0:T(1024)(128)(2,1)S(1)} %get-tuple-element.87, ...), channel_id=2, replica_groups=mesh['shard'=8,'tensor'=4] {'shard'}, use_global_device_ids=true, to_apply=%region_32.33.clone | all-reduce | flops 10240 | bytes 40960
  1096.0 11.8 %pad_maximum_fusion = f32[2048,2048]{1,0:T(8,128)} fusion(f32[1024,2048]{1,0:T(8,128)} %get-tuple-element.103, f32[1024,2048]{1,0:T(8,128)} %get-tuple-element.104), kind=kLoop, calls=%fused_computation.2 | loop fusion | flops 4194304 | bytes 33554432 | tf_op jit(solution)/shard_map/concatenate | solution.py:354
  (319 shorter events, 242.3 us)
Async XLA Ops:
  7.2 43.0 %copy-start.45 = (bf16[2048]{0:T(1024)(128)(2,1)S(1)}, bf16[2048]{0:T(1024)(128)(2,1)}, u32[]{:S(2)}) copy-start(bf16[2048]{0:T(1024)(128)(2,1)} %param.24) | copy-start | bytes 12292
  7.2 43.6 %copy-start.47 = (bf16[2,3,256]{2,0,1:T(2,128)(2,1)S(1)}, bf16[2,3,256]{2,0,1:T(2,128)(2,1)}, u32[]{:S(2)}) copy-start(bf16[2,3,256]{2,0,1:T(2,128)(2,1)} %param.18) | copy-start | bytes 9220
  7.2 53.1 %all-gather.13.cloned.1.call-start = ((), (), s32[]{:S(2)}) async-start(), calls=%async_computation.5 | async-start | bytes 2359296 | tf_op jit(solution)/shard_map/all_gather | solution.py:301
  9.0 80.0 %all-gather.11.cloned.1.call-start = ((), (), s32[]{:S(2)}) async-start(), calls=%async_computation.4 | async-start | bytes 7077888 | tf_op jit(solution)/shard_map/all_gather | solution.py:300
  11.2 209.7 %all-gather.15.cloned.1.call-start = ((), (), s32[]{:S(2)}) async-start(), calls=%async_computation.6 | async-start | bytes 9437184 | tf_op jit(solution)/shard_map/all_gather | solution.py:302
  11.9 241.2 %all-gather.17.cloned.1.call-start = ((), (), s32[]{:S(2)}) async-start(), calls=%async_computation.7 | async-start | bytes 9437184 | tf_op jit(solution)/shard_map/all_gather | solution.py:303
  12.5 486.9 %reduce-scatter.7.cloned.1.call-start = ((), (), s32[]{:S(2)}) async-start(), calls=%async_computation.9 | async-start | bytes 2359296 | tf_op jit(solution)/shard_map/reduce_scatter | solution.py:349
  50.2 155.3 %copy-start.39 = (f32[8,1,256]{2,1,0:T(1,128)}, f32[8,1,256]{2,1,0:T(1,128)S(1)}, u32[]{:S(2)}) copy-start(f32[8,1,256]{2,1,0:T(1,128)S(1)} %convert_element_type.304) | copy-start | bytes 24580
  177.8 371.8 %reduce-scatter.5.cloned.1.call-start = ((), (), s32[]{:S(2)}) async-start(), calls=%async_computation.8 | async-start | bytes 7077888 | tf_op jit(solution)/shard_map/reduce_scatter | solution.py:349
  220.8 331.9 %reduce-scatter.9.cloned.1.call-start = ((), (), s32[]{:S(2)}) async-start(), calls=%async_computation.10 | async-start | bytes 9437184 | tf_op jit(solution)/shard_map/reduce_scatter | solution.py:349
  271.5 33.4 %slice-start.2 = ((s8[8388608]{0:T(1024)(128)(4,1)}), s8[4194304]{0:T(1024)(128)(4,1)S(1)}, s32[]{:S(2)}) async-start(s8[8388608]{0:T(1024)(128)(4,1)} %bitcast.170), calls=%async_computation.15 | async-start | bytes 8388608
  321.8 233.7 %reduce-scatter.11.cloned.1.call-start = ((), (), s32[]{:S(2)}) async-start(), calls=%async_computation.11 | async-start | bytes 9437184 | tf_op jit(solution)/shard_map/reduce_scatter | solution.py:349
  321.8 25.1 %slice-start.8 = ((s8[8388608]{0:T(1024)(128)(4,1)}), s8[4194304]{0:T(1024)(128)(4,1)S(1)}, s32[]{:S(2)}) async-start(s8[8388608]{0:T(1024)(128)(4,1)} %bitcast.176), calls=%async_computation.21 | async-start | bytes 8388608
  375.1 664.3 %all-reduce.11.cloned.1.call-start = ((), (), s32[]{:S(2)}) async-start(), calls=%async_computation.12 | async-start | bytes 33554432 | tf_op jit(solution)/shard_map/psum | solution.py:314
  390.2 30.3 %copy-start.61 = (bf16[1024,2048]{1,0:T(8,128)(2,1)S(1)}, bf16[1024,2048]{1,0:T(8,128)(2,1)}, u32[]{:S(2)}) copy-start(bf16[1024,2048]{1,0:T(8,128)(2,1)} %get-tuple-element.135) | copy-start | bytes 12582916
  433.0 27.7 %slice-start.4 = ((s8[8388608]{0:T(1024)(128)(4,1)}), s8[4194304]{0:T(1024)(128)(4,1)S(1)}, s32[]{:S(2)}) async-start(s8[8388608]{0:T(1024)(128)(4,1)} %bitcast.172), calls=%async_computation.17 | async-start | bytes 8388608
  433.1 27.7 %slice-start.14 = ((s8[8388608]{0:T(1024)(128)(4,1)}), s8[4194304]{0:T(1024)(128)(4,1)S(1)}, s32[]{:S(2)}) async-start(s8[8388608]{0:T(1024)(128)(4,1)} %bitcast.196), calls=%async_computation.27 | async-start | bytes 8388608
  437.4 23.3 %slice-start.5 = ((s8[8388608]{0:T(1024)(128)(4,1)}), s8[4194304]{0:T(1024)(128)(4,1)S(1)}, s32[]{:S(2)}) async-start(s8[8388608]{0:T(1024)(128)(4,1)} %bitcast.172), calls=%async_computation.18 | async-start | bytes 8388608
  437.4 23.3 %slice-start.15 = ((s8[8388608]{0:T(1024)(128)(4,1)}), s8[4194304]{0:T(1024)(128)(4,1)S(1)}, s32[]{:S(2)}) async-start(s8[8388608]{0:T(1024)(128)(4,1)} %bitcast.196), calls=%async_computation.28 | async-start | bytes 8388608
  477.3 19.1 %copy-start.8 = (f32[4,256,2,256]{3,1,0,2:T(8,128)S(1)}, f32[4,256,2,256]{3,1,0,2:T(8,128)}, u32[]{:S(2)}) copy-start(f32[4,256,2,256]{3,1,0,2:T(8,128)} %copy.133) | copy-start | bytes 6291460
  479.2 19.8 %copy-start.12 = (f32[4,256,2,256]{3,1,0,2:T(8,128)S(1)}, f32[4,256,2,256]{3,1,0,2:T(8,128)}, u32[]{:S(2)}) copy-start(f32[4,256,2,256]{3,1,0,2:T(8,128)} %copy-done.11) | copy-start | bytes 6291460
  479.2 19.8 %copy-start.14 = (f32[4,256,2,256]{3,1,0,2:T(8,128)S(1)}, f32[4,256,2,256]{3,1,0,2:T(8,128)}, u32[]{:S(2)}) copy-start(f32[4,256,2,256]{3,1,0,2:T(8,128)} %copy-done.13) | copy-start | bytes 6291460
  479.2 19.8 %copy-start.16 = (f32[4,256,2,256]{3,1,0,2:T(8,128)S(1)}, f32[4,256,2,256]{3,1,0,2:T(8,128)}, u32[]{:S(2)}) copy-start(f32[4,256,2,256]{3,1,0,2:T(8,128)} %copy-done.15) | copy-start | bytes 6291460
  1075.3 32.5 %copy-start.46 = (f32[256]{0:T(256)}, f32[256]{0:T(256)S(1)}, u32[]{:S(2)}) copy-start(f32[256]{0:T(256)S(1)} %dynamic-slice_convert_fusion.2) | copy-start | bytes 3076
  (66 other events, 444.1 us)
Sparse Core Ops, SparseCore 0:
  10.5 30.5 all-gather.12
  43.6 45.3 all-gather.10
  90.9 54.2 all-gather.14
  146.9 54.2 all-gather.16
  204.3 41.1 reduce-scatter.6
  248.7 61.5 reduce-scatter.4
  321.9 71.3 reduce-scatter.8
  396.8 71.2 reduce-scatter.10
  477.4 562.0 all-reduce.10
where the time goes:
time: 1120 us
  waiting for transfers between devices  500 us (45%)
  matrix products  340 us (30%)
  blocking collectives  125 us (11%)
  other arithmetic  87.2 us (8%)
  local copies, waits for them, and re-layouts  47.4 us (4%)
  between operations  16.2 us (1%)
    psum x1, waiting for transfers between devices, per_device(): lax.psum(partial_value.astype(jnp.bfloat16), 'tensor').astype(jnp.float32)  481 us
    dot_general x2, matrix products, backward_pass(): jnp.einsum('mf,df->md', d_pre_b, fc1_full, preferred_element_type=jnp.flo...  45.1 us
    dot_general x2, matrix products, backward_pass(): jnp.dot(grad_block, fc2_full, preferred_element_type=jnp.float32)  35 us
    dot_general x2, matrix products, backward_pass(): jnp.einsum('md,mf->df', normed_two, d_pre_b, preferred_element_type=jnp.f...  33.6 us
    dot_general x2, matrix products, backward_pass(): jnp.einsum('md,mhkc->dhkc', normed_one, d_qkv_b, preferred_element_type=j...  30 us
    dot_general x2, matrix products, forward_pass(): jnp.dot(normed_two, fc1_full, preferred_element_type=jnp.float32)  28.4 us
    unnamed x180, local copies, waits for them, and re-layouts  28.2 us
    dot_general x2, matrix products, backward_pass(): jnp.einsum('md,mf->df', grad_block, hidden, preferred_element_type=jnp.fl...  28.2 us
  transfers between devices with their start and end apart: 9, of which 2 were waited for; matrix products, arithmetic and copies ran while one was open for 37% of the time, Pallas kernels for 0%

commit v1 on v0

v1 whole, which is shorter than its diff:
```python
import functools
import math

import jax
import jax.numpy as jnp
from jax import lax
from jax.experimental import pallas as pl
from jax.experimental.pallas import tpu as pltpu
from jax.sharding import PartitionSpec as P


ROT = 64
SEQ = 256
CORES = 2
LANES = 128
FWD_PARTS = (4, 4, 4, 4)
BWD_PARTS = (4, 4, 4, 4)
LAST_PARTS = (1,)
VMEM_LIMIT = 60 << 20


NORM_EPS = 1e-05
ROOT_HALF = 0.7071067811865476
INV_ROOT_TWO_PI = 0.3989422804014327
MESH = pl.DeviceIdType.MESH


def normalize(residual):
    row_mean = jnp.mean(residual, axis=-1, keepdims=True)
    centered = residual - row_mean
    row_var = jnp.mean(centered * centered, axis=-1, keepdims=True)
    inv_std = lax.rsqrt(row_var + NORM_EPS)
    return (centered * inv_std, inv_std)


def norm_backward(grad_normed, gain_wide, normalized, inv_std):
    scaled_grad = grad_normed * gain_wide
    return inv_std * (
        scaled_grad
        - jnp.mean(scaled_grad, axis=-1, keepdims=True)
        - normalized * jnp.mean(scaled_grad * normalized, axis=-1, keepdims=True)
    )


def gelu_exact(pre_act):
    return 0.5 * pre_act * (1.0 + lax.erf(pre_act * ROOT_HALF))


def gelu_slope(pre_act):
    return (
        0.5 * (1.0 + lax.erf(pre_act * ROOT_HALF))
        + pre_act * jnp.exp(-0.5 * pre_act * pre_act) * INV_ROOT_TWO_PI
    )


def rotary_tables(length, rot_dims):
    half_dims = rot_dims // 2
    frequency = jnp.power(10000.0, -2.0 * jnp.arange(half_dims, dtype=jnp.float32) / rot_dims)
    angles = jnp.arange(length, dtype=jnp.float32)[:, None] * frequency[None, :]
    cos_tab, sin_tab = jnp.cos(angles), jnp.sin(angles)
    zeros = jnp.zeros((length, half_dims), jnp.float32)
    rest = jnp.zeros((length, LANES - rot_dims), jnp.float32)
    keep = jnp.concatenate([cos_tab, cos_tab, rest + 1.0], axis=1)
    from_upper = jnp.concatenate([-sin_tab, zeros, rest], axis=1)
    from_lower = jnp.concatenate([zeros, sin_tab, rest], axis=1)
    return jnp.stack([keep, from_upper, from_lower])


def rotate(field, table_ref, sign):
    first = field[:, :LANES]
    half_dims = ROT // 2
    turned = (
        first * table_ref[0]
        + sign * pltpu.roll(first, LANES - half_dims, 1) * table_ref[1]
        + sign * pltpu.roll(first, half_dims, 1) * table_ref[2]
    )
    return jnp.concatenate([turned, field[:, LANES:]], axis=1)


def dot_nn(left, right):
    return jnp.dot(left, right, preferred_element_type=jnp.float32)


def dot_nt(left, right):
    return lax.dot_general(left, right, (((1,), (1,)), ((), ())), preferred_element_type=jnp.float32)


def dot_tn(left, right):
    return lax.dot_general(left, right, (((0,), (0,)), ((), ())), preferred_element_type=jnp.float32)


def probabilities(queries, key_rows, score_scale):
    scores = dot_nt(queries, key_rows) * score_scale
    length = scores.shape[0]
    row_at = lax.broadcasted_iota(jnp.int32, (length, length), 0)
    key_at = lax.broadcasted_iota(jnp.int32, (length, length), 1)
    scores = jnp.where(row_at >= key_at, scores, -1e30)
    row_top = jnp.max(scores, axis=-1, keepdims=True)
    weights = jnp.exp(scores - row_top)
    return weights * (1.0 / jnp.sum(weights, axis=-1, keepdims=True))


def call(kernel, grid, in_specs, out_specs, out_shape, flops, moved, **more):
    return pl.pallas_call(
        kernel,
        grid=grid,
        in_specs=in_specs,
        out_specs=out_specs,
        out_shape=out_shape,
        compiler_params=pltpu.CompilerParams(vmem_limit_bytes=VMEM_LIMIT),
        cost_estimate=pl.CostEstimate(flops=flops, bytes_accessed=moved, transcendentals=0),
        **more,
    )


def whole(shape):
    return pl.BlockSpec(
        shape, lambda step: (0,) * len(shape), pipeline_mode=pl.Buffered(1)
    )


def by_rows(rows, columns, first=0):
    return pl.BlockSpec((rows, columns), lambda step: (step + first, 0))


def attention_block(
    x_ref,
    vec_ref,
    weight_ref,
    shift_ref,
    table_ref,
    one_ref,
    two_ref,
    qkv_ref,
    attn_ref,
    head_count,
    head_dim,
):
    score_scale = 1.0 / math.sqrt(head_dim)
    normalized, _ = normalize(x_ref[...].astype(jnp.float32))
    one = (normalized * vec_ref[0:1] + vec_ref[1:2]).astype(jnp.bfloat16)
    one_ref[...] = one
    two_ref[...] = (normalized * vec_ref[2:3] + vec_ref[3:4]).astype(jnp.bfloat16)
    for head in range(head_count):
        fields = []
        for kind in range(3):
            at = slice((head * 3 + kind) * head_dim, (head * 3 + kind + 1) * head_dim)
            field = dot_nn(one, weight_ref[:, at]) + shift_ref[:, at]
            if kind < 2:
                field = rotate(field, table_ref, 1.0)
            field = field.astype(jnp.bfloat16)
            qkv_ref[:, at] = field
            fields.append(field)
        probs = probabilities(fields[0], fields[1], score_scale).astype(jnp.bfloat16)
        attn_ref[:, head * head_dim : (head + 1) * head_dim] = dot_nn(probs, fields[2]).astype(
            jnp.bfloat16
        )


def attention_forward(tokens, vectors, qkv_full, qkv_shift, table, head_count, head_dim):
    row_count, width = tokens.shape
    qkv_width = qkv_full.shape[1]

    def kernel(x_ref, vec_ref, weight_ref, shift_ref, table_ref, *out_refs):
        attention_block(
            x_ref, vec_ref, weight_ref, shift_ref, table_ref, *out_refs, head_count, head_dim
        )

    attn_width = head_count * head_dim
    return call(
        kernel,
        (row_count // SEQ,),
        [
            by_rows(SEQ, width),
            whole(vectors.shape),
            whole(qkv_full.shape),
            whole(qkv_shift.shape),
            whole(table.shape),
        ],
        [
            by_rows(SEQ, width),
            by_rows(SEQ, width),
            by_rows(SEQ, qkv_width),
            by_rows(SEQ, attn_width),
        ],
        [
            jax.ShapeDtypeStruct((row_count, width), jnp.bfloat16),
            jax.ShapeDtypeStruct((row_count, width), jnp.bfloat16),
            jax.ShapeDtypeStruct((row_count, qkv_width), jnp.bfloat16),
            jax.ShapeDtypeStruct((row_count, attn_width), jnp.bfloat16),
        ],
        2 * row_count * width * qkv_width,
        2 * (3 * row_count * width + width * qkv_width + row_count * (qkv_width + attn_width)),
        name="attention_forward",
    )(tokens, vectors, qkv_full, qkv_shift, table)


def attention_backward(cotangent, out_full, qkv, table, head_count, head_dim):
    row_count, width = cotangent.shape
    qkv_width = qkv.shape[1]
    attn_width = head_count * head_dim
    score_scale = 1.0 / math.sqrt(head_dim)

    def kernel(grad_ref, out_ref, qkv_ref, table_ref, d_qkv_ref, shift_ref, sum_ref):
        @pl.when(pl.program_id(0) == 0)
        def _():
            shift_ref[...] = jnp.zeros_like(shift_ref)
            sum_ref[...] = jnp.zeros_like(sum_ref)

        grad = grad_ref[...]
        sum_ref[0:1] += jnp.sum(grad.astype(jnp.float32), axis=0, keepdims=True)
        for head in range(head_count):
            d_attn = dot_nn(grad, out_ref[:, head * head_dim : (head + 1) * head_dim])
            d_attn = d_attn.astype(jnp.bfloat16)
            at = [
                slice((head * 3 + kind) * head_dim, (head * 3 + kind + 1) * head_dim)
                for kind in range(3)
            ]
            queries, key_rows, values = (qkv_ref[:, part] for part in at)
            probs = probabilities(queries, key_rows, score_scale)
            d_values = dot_tn(probs.astype(jnp.bfloat16), d_attn)
            d_probs = dot_nt(d_attn, values)
            row_delta = jnp.sum(probs * d_probs, axis=-1, keepdims=True)
            d_scores = (probs * (d_probs - row_delta) * score_scale).astype(jnp.bfloat16)
            d_queries = rotate(dot_nn(d_scores, key_rows), table_ref, -1.0)
            d_keys = rotate(dot_tn(d_scores, queries), table_ref, -1.0)
            for part, value in zip(at, (d_queries, d_keys, d_values)):
                d_qkv_ref[:, part] = value.astype(jnp.bfloat16)
                shift_ref[0:1, part] += jnp.sum(value, axis=0, keepdims=True)

    return call(
        kernel,
        (row_count // SEQ,),
        [by_rows(SEQ, width), whole(out_full.shape), by_rows(SEQ, qkv_width), whole(table.shape)],
        [
            by_rows(SEQ, qkv_width),
            pl.BlockSpec((8, qkv_width), lambda step: (0, 0)),
            pl.BlockSpec((8, width), lambda step: (0, 0)),
        ],
        [
            jax.ShapeDtypeStruct((row_count, qkv_width), jnp.bfloat16),
            jax.ShapeDtypeStruct((8, qkv_width), jnp.float32),
            jax.ShapeDtypeStruct((8, width), jnp.float32),
        ],
        2 * row_count * width * attn_width + 10 * row_count * SEQ * attn_width,
        2 * (row_count * width + width * attn_width + 2 * row_count * qkv_width),
        name="attention_backward",
    )(cotangent, out_full, qkv, table)


def branch_part(attn_out, hidden, out_full, fc2_full, first, rows):
    width = out_full.shape[0]

    def kernel(attn_ref, hidden_ref, out_ref, fc2_ref, part_ref):
        total = dot_nt(attn_ref[...], out_ref[...]) + dot_nt(hidden_ref[...], fc2_ref[...])
        part_ref[...] = total.astype(jnp.bfloat16)

    inner = attn_out.shape[1] + hidden.shape[1]
    return call(
        kernel,
        (rows // SEQ,),
        [
            by_rows(SEQ, attn_out.shape[1], first // SEQ),
            by_rows(SEQ, hidden.shape[1], first // SEQ),
            whole(out_full.shape),
            whole(fc2_full.shape),
        ],
        by_rows(SEQ, width),
        jax.ShapeDtypeStruct((rows, width), jnp.bfloat16),
        2 * rows * width * inner,
        2 * (rows * (width + inner) + width * inner),
        name="branch_part",
    )(attn_out, hidden, out_full, fc2_full)


def input_grad(d_pre, d_qkv, tokens, vectors, fc1_full, qkv_full, first, rows):
    width = tokens.shape[1]

    def kernel(pre_ref, qkv_ref, x_ref, vec_ref, fc1_ref, weight_ref, grad_ref, terms_ref):
        @pl.when(pl.program_id(0) == 0)
        def _():
            terms_ref[...] = jnp.zeros_like(terms_ref)

        normalized, inv_std = normalize(x_ref[...].astype(jnp.float32))
        d_one = dot_nt(qkv_ref[...], weight_ref[...])
        terms_ref[0:1] += jnp.sum(d_one * normalized, axis=0, keepdims=True)
        terms_ref[1:2] += jnp.sum(d_one, axis=0, keepdims=True)
        d_two = dot_nt(pre_ref[...], fc1_ref[...])
        terms_ref[2:3] += jnp.sum(d_two * normalized, axis=0, keepdims=True)
        terms_ref[3:4] += jnp.sum(d_two, axis=0, keepdims=True)
        joined = d_one * vec_ref[0:1] + d_two * vec_ref[2:3]
        grad_ref[...] = norm_backward(joined, 1.0, normalized, inv_std).astype(jnp.bfloat16)

    inner = d_pre.shape[1] + d_qkv.shape[1]
    return call(
        kernel,
        (rows // SEQ,),
        [
            by_rows(SEQ, d_pre.shape[1], first // SEQ),
            by_rows(SEQ, d_qkv.shape[1], first // SEQ),
            by_rows(SEQ, width, first // SEQ),
            whole(vectors.shape),
            whole(fc1_full.shape),
            whole(qkv_full.shape),
        ],
        [by_rows(SEQ, width), pl.BlockSpec((8, width), lambda step: (0, 0))],
        [
            jax.ShapeDtypeStruct((rows, width), jnp.bfloat16),
            jax.ShapeDtypeStruct((8, width), jnp.float32),
        ],
        2 * rows * width * inner,
        2 * (rows * (2 * width + inner) + width * inner),
        name="input_grad",
    )(d_pre, d_qkv, tokens, vectors, fc1_full, qkv_full)


def chip_at(place, chips):
    if chips & (chips - 1):
        return place
    chip, bit = 0, 1
    while bit < chips:
        chip = chip + bit * lax.rem(place // bit + place // (2 * bit), 2)
        bit *= 2
    return chip


def place_of(chip, chips):
    if chips & (chips - 1):
        return chip
    place, bit = 0, 1
    while bit < chips:
        ones, higher = 0, bit
        while higher < chips:
            ones = ones + chip // higher
            higher *= 2
        place = place + bit * lax.rem(ones, 2)
        bit *= 2
    return place


def ring_serves(shards):
    chips = shards // CORES
    return shards % CORES == 0 and chips % 2 == 0 and chips >= 4


def gather_forward(parts, tokens, qkv_shift, fc1_shift, table, shards, head_count, head_dim):
    chips = shards // CORES
    count = len(parts)
    hops = chips // 2 - 1
    kinds = 2 * hops + 2
    total_kinds = kinds + 1 + kinds
    row_count, width = tokens.shape
    own_rows, qkv_width = parts[1].shape
    units = parts[2].shape[1]
    attn_width = head_count * head_dim

    def kernel(*refs):
        own = refs[:count]
        x_ref, qkv_shift_ref, fc1_shift_ref, table_ref = refs[count : count + 4]
        full = refs[count + 4 : 2 * count + 4]
        one_ref, two_ref, qkv_ref, attn_ref, hidden_ref, pre_ref = refs[2 * count + 4 : 2 * count + 10]
        vec_buf, vec_rows, qkv_buf, fc1_buf, send_sems, recv_sems, keep_sems, load_sems = refs[
            2 * count + 10 :
        ]
        me = lax.axis_index("shard")
        core = lax.rem(me, CORES)
        place = place_of(me // CORES, chips)

        def shard_at(shift, flip=0):
            there = chip_at(lax.rem(place + shift + chips, chips), chips)
            return there * CORES + (1 - core if flip else core)

        right, left, peer = shard_at(1), shard_at(-1), shard_at(0, 1)
        barrier = pltpu.get_barrier_semaphore()
        for target in (right, left, peer):
            pl.semaphore_signal(barrier, inc=1, device_id={"shard": target}, device_id_type=MESH)
        pl.semaphore_wait(barrier, 3)
        copies = {}

        def send(index, kind, src, dst, target):
            copy = pltpu.make_async_remote_copy(
                src_ref=src,
                dst_ref=dst,
                send_sem=send_sems.at[index, kind],
                recv_sem=recv_sems.at[index, kind],
                device_id={"shard": target},
                device_id_type=MESH,
            )
            copy.start()
            copies[index, kind] = copy

        def half(which, index):
            rows = own[index].shape[0] // 2
            return pl.ds(which * rows, rows)

        def across(index, kind, piece):
            send(index, kinds + 1 + kind, piece, piece, peer)

        def keep(index):
            return pltpu.make_async_copy(own[index], full[index].at[me], keep_sems.at[index])

        def begin(*indices):
            for index in indices:
                mine = full[index].at[me]
                send(index, 0, own[index], mine, right)
                send(index, hops, own[index], mine, left)
                send(index, kinds, own[index], mine, peer)
                keep(index).start()

        def forward(*indices):
            for hop in range(hops):
                for index in indices:
                    for kind, sign, target in ((hop, -1, right), (hops + hop, 1, left)):
                        copies[index, kind].wait_recv()
                        shard = shard_at(sign * (hop + 1))
                        piece = full[index].at[shard]
                        if hop + 1 < hops:
                            send(index, kind + 1, piece, piece, target)
                        else:
                            which = 0 if sign < 0 else 1
                            part = full[index].at[shard, half(which, index)]
                            send(index, 2 * hops + which, part, part, target)
                        across(index, kind, piece)

        def finish(*indices):
            for index in indices:
                for which in range(2):
                    last = 2 * hops + which
                    copies[index, last].wait_recv()
                    across(index, last, full[index].at[shard_at(chips // 2), half(which, index)])
            for index in indices:
                for kind in range(kinds, total_kinds):
                    copies[index, kind].wait_recv()
                for kind in range(total_kinds):
                    copies[index, kind].wait_send()
                keep(index).wait()

        def load(index, buffer, slot):
            loads = [
                pltpu.make_async_copy(
                    full[index].at[shard],
                    buffer.at[pl.ds(shard * own[index].shape[0], own[index].shape[0])],
                    load_sems.at[slot + shard],
                )
                for shard in range(shards)
            ]
            for one in loads:
                one.start()
            for one in loads:
                one.wait()

        def rows_of(columns):
            return pl.BlockSpec((SEQ, columns), lambda step: (step, 0))

        begin(0, 1)
        forward(0, 1)
        begin(2, 3)
        finish(0, 1)
        load(0, vec_buf, 0)
        load(1, qkv_buf, shards)
        for shard in range(shards):
            vec_rows[:, shard * own_rows : (shard + 1) * own_rows] = vec_buf[
                shard * 16 : (shard + 1) * 16
            ].astype(jnp.float32)

        def attend(*blocks):
            attention_block(
                blocks[0],
                vec_rows,
                qkv_buf,
                qkv_shift_ref,
                table_ref,
                *blocks[1:],
                head_count,
                head_dim,
            )

        pltpu.emit_pipeline(
            attend,
            grid=(row_count // SEQ,),
            in_specs=[rows_of(width)],
            out_specs=[rows_of(width), rows_of(width), rows_of(qkv_width), rows_of(attn_width)],
        )(x_ref, one_ref, two_ref, qkv_ref, attn_ref)

        forward(2, 3)
        begin(4)
        finish(2)
        load(2, fc1_buf, 2 * shards)

        def feed(two_block, hidden_block, pre_block):
            tile = min(units, 512)
            for at in range(0, units, tile):
                cut = slice(at, at + tile)
                pre = dot_nn(two_block[...], fc1_buf[:, cut]) + fc1_shift_ref[:, cut]
                pre_block[:, cut] = pre
                hidden_block[:, cut] = gelu_exact(pre).astype(jnp.bfloat16)

        pltpu.emit_pipeline(
            feed,
            grid=(row_count // SEQ,),
            in_specs=[rows_of(width)],
            out_specs=[rows_of(units), rows_of(units)],
        )(two_ref, hidden_ref, pre_ref)

        forward(4)
        finish(3, 4)

    sent = sum(part.size * part.dtype.itemsize for part in parts)
    any_space = pl.BlockSpec(memory_space=pl.ANY)
    in_vmem = pl.BlockSpec(memory_space=pltpu.VMEM)
    shapes = [((shards,) + part.shape, part.dtype) for part in parts] + [
        ((row_count, width), jnp.bfloat16),
        ((row_count, width), jnp.bfloat16),
        ((row_count, qkv_width), jnp.bfloat16),
        ((row_count, attn_width), jnp.bfloat16),
        ((row_count, units), jnp.bfloat16),
        ((row_count, units), jnp.float32),
    ]
    results = pl.pallas_call(
        kernel,
        in_specs=[in_vmem] * count + [any_space] + [in_vmem] * 3,
        out_specs=[any_space] * len(shapes),
        out_shape=[jax.ShapeDtypeStruct(*shape) for shape in shapes],
        scratch_shapes=[
            pltpu.VMEM((shards * 16, own_rows), jnp.bfloat16),
            pltpu.VMEM((16, width), jnp.float32),
            pltpu.VMEM((width, qkv_width), jnp.bfloat16),
            pltpu.VMEM((width, units), jnp.bfloat16),
            pltpu.SemaphoreType.DMA((count, total_kinds)),
            pltpu.SemaphoreType.DMA((count, total_kinds)),
            pltpu.SemaphoreType.DMA((count,)),
            pltpu.SemaphoreType.DMA((3 * shards,)),
        ],
        compiler_params=pltpu.CompilerParams(
            collective_id=0, has_side_effects=True, vmem_limit_bytes=VMEM_LIMIT
        ),
        cost_estimate=pl.CostEstimate(
            flops=2 * row_count * width * (qkv_width + units),
            bytes_accessed=2 * shards * sent + 18 * row_count * width,
            transcendentals=row_count * units,
        ),
        name="gather_forward",
    )(*parts, tokens, qkv_shift, fc1_shift, table)
    return results[:count], results[count:]


def line_sum(part, count):
    if count == 1:
        return part
    if count % 2:
        return lax.psum(part, "tensor")
    me = lax.axis_index("tensor")
    middle = count // 2
    total = part
    for step in range(count - 1):
        if step < middle:
            moves = [(step, step + 1), (count - 1 - step, count - 2 - step)]
        else:
            near = count - 2 - step
            moves = [(near + 1, near), (count - 2 - near, count - 1 - near)]
        arrived = lax.ppermute(total, "tensor", moves)
        if step < middle:
            total = lax.optimization_barrier(total + arrived)
        else:
            total = jnp.where((me == near) | (me == count - 1 - near), arrived, total)
            if step < count - 2:
                total = lax.optimization_barrier(total)
    return total


def per_device(
    shards,
    tensors,
    tokens,
    ln1_gain,
    ln1_bias,
    qkv_weight,
    qkv_bias,
    out_weight,
    out_bias,
    ln2_gain,
    ln2_bias,
    fc1_weight,
    fc1_bias,
    fc2_weight,
    fc2_bias,
    cotangent,
):
    own_rows, head_count, kinds, head_dim = qkv_weight.shape
    row_count, width = tokens.shape
    table = rotary_tables(SEQ, ROT)

    vectors = jnp.stack([ln1_gain, ln1_bias, ln2_gain, ln2_bias, out_bias, fc2_bias] + [ln1_gain] * 10)
    parts = [
        vectors,
        qkv_weight.reshape(own_rows, -1),
        fc1_weight,
        out_weight.reshape(own_rows, -1),
        fc2_weight,
    ]
    qkv_shift = qkv_bias.astype(jnp.float32).reshape(1, -1)
    fc1_shift = fc1_bias.astype(jnp.float32).reshape(1, -1)
    forward = None
    if ring_serves(shards):
        gathered, forward = gather_forward(
            parts, tokens, qkv_shift, fc1_shift, table, shards, head_count, head_dim
        )
    else:
        gathered = [lax.all_gather(part, "shard") for part in parts]
    vectors = gathered[0].astype(jnp.float32).transpose(1, 0, 2).reshape(16, width)
    qkv_full, fc1_full, out_full, fc2_full = (
        part.reshape(width, part.shape[-1]) for part in gathered[1:]
    )
    if forward is None:
        normed_one, normed_two, qkv, attn_out = attention_forward(
            tokens, vectors, qkv_full, qkv_shift, table, head_count, head_dim
        )
        pre_act = dot_nn(normed_two, fc1_full) + fc1_shift
        hidden = gelu_exact(pre_act).astype(jnp.bfloat16)
    else:
        normed_one, normed_two, qkv, attn_out, hidden, pre_act = forward

    block_out = lax.optimization_barrier(jnp.zeros((row_count, width), jnp.bfloat16))
    start = 0
    shifts = vectors[4] + vectors[5]
    for parts in FWD_PARTS:
        rows = row_count // parts
        partial_value = branch_part(attn_out, hidden, out_full, fc2_full, start, rows)
        branch_total = line_sum(partial_value, tensors).astype(jnp.float32)
        out_rows = tokens[start : start + rows].astype(jnp.float32) + branch_total + shifts
        block_out = lax.dynamic_update_slice(block_out, out_rows.astype(jnp.bfloat16), (start, 0))
        start += rows

    def weight_grad(left, right):
        return dot_tn(left, right).astype(jnp.bfloat16)

    def scattered(left, right):
        grad = weight_grad(left, right)
        grad = lax.psum_scatter(grad, "shard", scatter_dimension=0, tiled=True)
        return grad.astype(jnp.float32)

    grad_fc2 = scattered(cotangent, hidden)
    grad_out = scattered(cotangent, attn_out)
    d_pre = dot_nn(cotangent, fc2_full) * gelu_slope(pre_act)
    fc1_shift_grad = jnp.sum(d_pre, axis=0)
    d_pre = d_pre.astype(jnp.bfloat16)
    grad_fc1 = scattered(normed_two, d_pre)
    d_qkv, qkv_shift_grad, shift_grad = attention_backward(
        cotangent, out_full, qkv, table, head_count, head_dim
    )
    grad_qkv = scattered(normed_one, d_qkv)

    grad_tokens = lax.optimization_barrier(jnp.zeros((row_count, width), jnp.float32))
    norm_terms = 0.0
    start = 0
    for index, parts in enumerate(BWD_PARTS):
        rows = row_count // parts
        d_input, terms = input_grad(d_pre, d_qkv, tokens, vectors, fc1_full, qkv_full, start, rows)
        norm_terms = norm_terms + terms
        at = 0
        for cut in LAST_PARTS if index + 1 == len(BWD_PARTS) else (1,):
            sent = rows // cut
            piece = lax.optimization_barrier(d_input[at : at + sent]) if cut > 1 else d_input
            summed = line_sum(piece, tensors).astype(jnp.float32)
            grad_rows = cotangent[start + at : start + at + sent].astype(jnp.float32) + summed
            grad_tokens = lax.dynamic_update_slice(grad_tokens, grad_rows, (start + at, 0))
            at += sent
        start += rows

    shared = lax.psum(
        jnp.concatenate(
            [norm_terms[:4].reshape(-1), shift_grad[0], qkv_shift_grad[0], fc1_shift_grad]
        ),
        "shard",
    )
    columns = shared[: 5 * width].reshape(5, shards, own_rows)
    columns = lax.dynamic_index_in_dim(columns, lax.axis_index("shard"), axis=1, keepdims=False)
    column_terms = line_sum(jnp.tile(columns[:4], (2, 1)), tensors)
    shared = shared[5 * width :]
    qkv_terms = shared[: head_count * kinds * head_dim].reshape(qkv_bias.shape)
    fc1_terms = shared[head_count * kinds * head_dim :]
    return (
        block_out,
        grad_tokens,
        column_terms[0],
        column_terms[1],
        grad_qkv.reshape(qkv_weight.shape),
        qkv_terms,
        grad_out.reshape(out_weight.shape),
        columns[4],
        column_terms[2],
        column_terms[3],
        grad_fc1,
        fc1_terms,
        grad_fc2,
        columns[4],
    )


def solution(mesh):
    return jax.shard_map(
        functools.partial(per_device, mesh.shape["shard"], mesh.shape["tensor"]),
        mesh=mesh,
        in_specs=(
            P("shard", None),
            P("shard"),
            P("shard"),
            P("shard", "tensor", None, None),
            P("tensor", None, None),
            P("shard", "tensor", None),
            P("shard"),
            P("shard"),
            P("shard"),
            P("shard", "tensor"),
            P("tensor"),
            P("shard", "tensor"),
            P("shard"),
            P("shard", None),
        ),
        out_specs=(
            P("shard", None),
            P("shard", None),
            P("shard"),
            P("shard"),
            P("shard", "tensor", None, None),
            P("tensor", None, None),
            P("shard", "tensor", None),
            P("shard"),
            P("shard"),
            P("shard"),
            P("shard", "tensor"),
            P("tensor"),
            P("shard", "tensor"),
            P("shard"),
        ),
        check_vma=False,
    )
```

time: 1120 us -> 1150 us (1.027)
  Pallas kernels: 0 us -> 275 us
  matrix products: 340 us -> 105 us
  blocking collectives: 125 us -> 24.3 us
  starting transfers between devices: 0.37 us -> 56.6 us
  waiting for transfers between devices: 500 us -> 535 us
    ppermute x0 -> x27, waiting for transfers between devices: none -> 535 us  [line_sum(): arrived = lax.ppermute(total, 'tensor', moves)]
    psum x1 -> x0, waiting for transfers between devices: 481 us -> none  [per_device(): lax.psum(partial_value.astype(jnp.bfloat16), 'tensor').astype(jnp.float32)]
    pallas_call x0 -> x10, Pallas kernels: none -> 275 us  [the longest x1 131 us: gather_forward(): pl.pallas_call(kernel, in_specs=[in_vmem] * count + [any_space] + [in_vme...]
    dot_general x36 -> x5, matrix products: 340 us -> 105 us  [the longest x4 75.4 us: dot_tn(): lax.dot_general(left, right, (((0,), (0,)), ((), ())), preferred_element_...]
    ppermute x0 -> x27, starting transfers between devices: none -> 55.6 us  [line_sum(): arrived = lax.ppermute(total, 'tensor', moves)]
    all_gather x6 -> x0, blocking collectives: 53.4 us -> none  [the longest x1 10.4 us: per_device(): lax.all_gather(own_shards[7], 'shard', axis=0, tiled=True)]
    add x7 -> x19, other arithmetic: 4.47 us -> 48.1 us  [the longest x18 48.1 us: line_sum(): total = lax.optimization_barrier(total + arrived)]
    convert_element_type x18 -> x1, other arithmetic: 34 us -> 2.79 us  [scattered(): return grad.astype(jnp.float32)]
  transfers between devices with their start and end apart: 9 -> 31, of which waited for: 2 -> 14; matrix products, arithmetic and copies ran while one was open for 37% -> 17% of each run, Pallas kernels for 0% -> 13%
where the time goes in v1:
time: 1150 us; the launch traced here: 1130 us
  waiting for transfers between devices  535 us (47%)
  Pallas kernels  275 us (24%)
  matrix products  105 us (9%)
  other arithmetic  84.4 us (7%)
  starting transfers between devices  56.6 us (5%)
  local copies, waits for them, and re-layouts  39.1 us (3%)
  blocking collectives  24.3 us (2%)
  between operations  14.9 us (1%)
    ppermute x27, waiting for transfers between devices, line_sum(): arrived = lax.ppermute(total, 'tensor', moves)  535 us
    pallas_call x1, Pallas kernels, gather_forward(): pl.pallas_call(kernel, in_specs=[in_vmem] * count + [any_space] + [in_vme...  131 us
    dot_general x4, matrix products, dot_tn(): lax.dot_general(left, right, (((0,), (0,)), ((), ())), preferred_element_...  75.4 us
    pallas_call x4, Pallas kernels, input_grad(): call(kernel, (rows // SEQ,), [by_rows(SEQ, d_pre.shape[1], first // SEQ),...  74 us
    ppermute x27, starting transfers between devices, line_sum(): arrived = lax.ppermute(total, 'tensor', moves)  55.6 us
    add x18, other arithmetic, line_sum(): total = lax.optimization_barrier(total + arrived)  48.1 us
    pallas_call x4, Pallas kernels, branch_part(): call(kernel, (rows // SEQ,), [by_rows(SEQ, attn_out.shape[1], first // SE...  46.6 us
    dot_general x1, matrix products, dot_nn(): return jnp.dot(left, right, preferred_element_type=jnp.float32)  29.5 us
  transfers between devices with their start and end apart: 31, of which 14 were waited for; matrix products, arithmetic and copies ran while one was open for 17% of the time, Pallas kernels for 13%

profile of v1, /device:TPU:0, one launch (start us, length us, event | category | flops | bytes accessed | tf_op | source)
XLA Modules:
  0.0 1133.9 jit_solution(708021338730638202)
XLA Ops:
  21.7 131.2 %gather_forward.1 = (bf16[8,16,256]{2,1,0:T(8,128)(2,1)}, bf16[8,256,1536]{2,1,0:T(8,128)(2,1)}, bf16[8,256,2048]{2,1,0:T(8,128)(2,1)}, bf16[8,256,512]{2,1,0:T(...) custom-call(bf16[16,256]{1,0:T(8,128)(2,1)} %stack.49.refs_0_, ...), custom_call_target="tpu_custom_call" | custom-call | flops 30064771072 | bytes 125960192 | tf_op jit(solution)/shard_map/gather_forward/pallas_call | solution.py:519
  163.2 22.9 %attention_backward.1 = (bf16[2048,1536]{1,0:T(8,128)(2,1)}, f32[8,1536]{1,0:T(8,128)}, f32[8,2048]{1,0:T(8,128)}) custom-call(bf16[2048,2048]{1,0:T(8,128)(2,1)} %grad_ref.1, bf16[2048,512]{1,0:T(8,128)(2,1)} %bitcast.66, bf16[2048,1536]{1,0:T(8,128)(2,1)} %get-tuple-element.42.qkv_ref, f32[3,256,128]{2,1,0:T(8,128)} %pad_maximum_fusion.refs_8_.table_ref), custom_call_target="tpu_custom_call" | custom-call | flops 6979321856 | bytes 23068672 | tf_op jit(solution)/shard_map/attention_backward/pallas_call | solution.py:231
  186.1 19.2 %convolution_convert_fusion.1 = bf16[2048,1536]{1,0:T(8,128)(2,1)} fusion(bf16[2048,2048]{1,0:T(8,128)(2,1)} %get-tuple-element.56, bf16[2048,1536]{1,0:T(8,128)(2,1)} %get-tuple-element.43.qkv_ref), kind=kOutput, calls=%fused_computation.8 | convolution fusion | flops 12888047616 | bytes 20971520 | tf_op jit(solution)/shard_map/dot_general | solution.py:89
  205.8 29.5 %fusion.14 = (f32[2048]{0:T(1024)S(1)}, bf16[2048,2048]{1,0:T(8,128)(2,1)S(1)}) fusion(f32[2048,2048]{1,0:T(8,128)} %get-tuple-element.41, bf16[2048,2048]{1,0:T(8,128)(2,1)} %grad_ref.1, bf16[2048,2048]{1,0:T(8,128)(2,1)} %bitcast.53), kind=kOutput, calls=%fused_computation.45 | convolution fusion | flops 17226004480 | bytes 41951232 | tf_op jit(solution)/shard_map/dot_general | solution.py:81
  238.7 22.2 %convolution_convert_fusion = bf16[2048,2048]{1,0:T(8,128)(2,1)} fusion(bf16[2048,2048]{1,0:T(8,128)(2,1)} %get-tuple-element.57, bf16[2048,2048]{1,0:T(8,128)(2,1)S(1)} %get-tuple-element.87.pre_ref), kind=kOutput, calls=%fused_computation.7 | convolution fusion | flops 17184063488 | bytes 25165824 | tf_op jit(solution)/shard_map/dot_general | solution.py:89
  262.5 17.6 %input_grad.7 = (bf16[512,2048]{1,0:T(8,128)(2,1)}, f32[8,2048]{1,0:T(8,128)}) custom-call(bf16[2048,2048]{1,0:T(8,128)(2,1)} %copy-done, bf16[2048,1536]{1,0:T(8,128)(2,1)} %get-tuple-element.43.qkv_ref, bf16[2048,2048]{1,0:T(8,128)(2,1)} %x_ref.7, f32[16,2048]{1,0:T(8,128)} %bitcast.74, bf16[2048,2048]{1,0:T(8,128)(2,1)} %bitcast.58, ...), custom_call_target="tpu_custom_call" | custom-call | flops 7516192768 | bytes 22544384 | tf_op jit(solution)/shard_map/input_grad/pallas_call | solution.py:295
  280.1 20.7 %input_grad.6 = (bf16[512,2048]{1,0:T(8,128)(2,1)}, f32[8,2048]{1,0:T(8,128)}) custom-call(bf16[2048,2048]{1,0:T(8,128)(2,1)} %copy-done, bf16[2048,1536]{1,0:T(8,128)(2,1)} %get-tuple-element.43.qkv_ref, bf16[2048,2048]{1,0:T(8,128)(2,1)} %x_ref.7, f32[16,2048]{1,0:T(8,128)} %bitcast.75, bf16[2048,2048]{1,0:T(8,128)(2,1)} %bitcast.59, ...), custom_call_target="tpu_custom_call" | custom-call | flops 7516192768 | bytes 22544384 | tf_op jit(solution)/shard_map/input_grad/pallas_call | solution.py:295
  300.8 17.9 %input_grad.5 = (bf16[512,2048]{1,0:T(8,128)(2,1)}, f32[8,2048]{1,0:T(8,128)}) custom-call(bf16[2048,2048]{1,0:T(8,128)(2,1)} %copy-done, bf16[2048,1536]{1,0:T(8,128)(2,1)} %get-tuple-element.43.qkv_ref, bf16[2048,2048]{1,0:T(8,128)(2,1)} %x_ref.7, f32[16,2048]{1,0:T(8,128)} %bitcast.76, bf16[2048,2048]{1,0:T(8,128)(2,1)} %bitcast.60, ...), custom_call_target="tpu_custom_call" | custom-call | flops 7516192768 | bytes 22544384 | tf_op jit(solution)/shard_map/input_grad/pallas_call | solution.py:295
  318.7 17.8 %input_grad.4 = (bf16[512,2048]{1,0:T(8,128)(2,1)}, f32[8,2048]{1,0:T(8,128)}) custom-call(bf16[2048,2048]{1,0:T(8,128)(2,1)} %copy-done, bf16[2048,1536]{1,0:T(8,128)(2,1)} %get-tuple-element.43.qkv_ref, bf16[2048,2048]{1,0:T(8,128)(2,1)} %x_ref.7, f32[16,2048]{1,0:T(8,128)} %bitcast.77, bf16[2048,2048]{1,0:T(8,128)(2,1)} %bitcast.61, ...), custom_call_target="tpu_custom_call" | custom-call | flops 7516192768 | bytes 22544384 | tf_op jit(solution)/shard_map/input_grad/pallas_call | solution.py:295
  339.1 24.3 %psum.7 = f32[13824]{0:T(1024)S(1)} all-reduce(f32[13824]{0:T(1024)S(1)} %pad_maximum_fusion.1), channel_id=1, replica_groups=mesh['shard'=8,'tensor'=4] {'shard'}, use_global_device_ids=true, to_apply=%region_1.2 | all-reduce | flops 13824 | bytes 110592 | tf_op jit(solution)/shard_map/psum | solution.py:670
  377.7 24.1 %convert_bitcast_fusion = bf16[2048,2048]{0,1:T(8,128)(2,1)} fusion(bf16[2048,2048]{1,0:T(8,128)(2,1)} %get-tuple-element.37.hidden_ref, bf16[2048,2048]{1,0:T(8,128)(2,1)} %grad_ref.1), kind=kOutput, calls=%fused_computation.6 | convolution fusion | flops 17184063488 | bytes 25165824 | tf_op jit(solution)/shard_map/dot_general | solution.py:89
  476.9 27.6 %collective-permute-done.15 = bf16[512,2048]{1,0:T(8,128)(2,1)} collective-permute-done((bf16[512,2048]{1,0:T(8,128)(2,1)S(1)}, bf16[512,2048]{1,0:T(8,128)(2,1)}, u32[]{:S(2)}, u32[]{:S(2)}) %collective-permute-start.15) | collective-permute-done | bytes 2097184 | tf_op jit(solution)/shard_map/ppermute | solution.py:561
  512.1 37.4 %collective-permute-done.12 = bf16[512,2048]{1,0:T(8,128)(2,1)} collective-permute-done((bf16[512,2048]{1,0:T(8,128)(2,1)}, bf16[512,2048]{1,0:T(8,128)(2,1)}, u32[]{:S(2)}, u32[]{:S(2)}) %collective-permute-start.12) | collective-permute-done | bytes 2097184 | tf_op jit(solution)/shard_map/ppermute | solution.py:561
  552.7 41.7 %collective-permute-done.9 = bf16[512,2048]{1,0:T(8,128)(2,1)} collective-permute-done((bf16[512,2048]{1,0:T(8,128)(2,1)}, bf16[512,2048]{1,0:T(8,128)(2,1)}, u32[]{:S(2)}, u32[]{:S(2)}) %collective-permute-start.9) | collective-permute-done | bytes 2097184 | tf_op jit(solution)/shard_map/ppermute | solution.py:561
  597.7 41.8 %collective-permute-done = bf16[512,2048]{1,0:T(8,128)(2,1)} collective-permute-done((bf16[512,2048]{1,0:T(8,128)(2,1)}, bf16[512,2048]{1,0:T(8,128)(2,1)}, u32[]{:S(2)}, u32[]{:S(2)}) %collective-permute-start) | collective-permute-done | bytes 2097184 | tf_op jit(solution)/shard_map/ppermute | solution.py:561
  642.6 41.7 %collective-permute-done.3 = bf16[512,2048]{1,0:T(8,128)(2,1)} collective-permute-done((bf16[512,2048]{1,0:T(8,128)(2,1)}, bf16[512,2048]{1,0:T(8,128)(2,1)}, u32[]{:S(2)}, u32[]{:S(2)}) %collective-permute-start.3) | collective-permute-done | bytes 2097184 | tf_op jit(solution)/shard_map/ppermute | solution.py:561
  687.5 38.2 %collective-permute-done.6 = bf16[512,2048]{1,0:T(8,128)(2,1)S(1)} collective-permute-done((bf16[512,2048]{1,0:T(8,128)(2,1)}, bf16[512,2048]{1,0:T(8,128)(2,1)S(1)}, u32[]{:S(2)}, u32[]{:S(2)}) %collective-permute-start.6) | collective-permute-done | bytes 2097184 | tf_op jit(solution)/shard_map/ppermute | solution.py:561
  780.1 20.3 %collective-permute-done.14 = bf16[512,2048]{1,0:T(8,128)(2,1)} collective-permute-done((bf16[512,2048]{1,0:T(8,128)(2,1)}, bf16[512,2048]{1,0:T(8,128)(2,1)}, u32[]{:S(2)}, u32[]{:S(2)}) %collective-permute-start.14) | collective-permute-done | bytes 2097184 | tf_op jit(solution)/shard_map/ppermute | solution.py:561
  815.6 29.7 %collective-permute-done.2 = bf16[512,2048]{1,0:T(8,128)(2,1)} collective-permute-done((bf16[512,2048]{1,0:T(8,128)(2,1)}, bf16[512,2048]{1,0:T(8,128)(2,1)}, u32[]{:S(2)}, u32[]{:S(2)}) %collective-permute-start.2) | collective-permute-done | bytes 2097184 | tf_op jit(solution)/shard_map/ppermute | solution.py:561
  850.6 39.7 %collective-permute-done.5 = bf16[512,2048]{1,0:T(8,128)(2,1)} collective-permute-done((bf16[512,2048]{1,0:T(8,128)(2,1)}, bf16[512,2048]{1,0:T(8,128)(2,1)}, u32[]{:S(2)}, u32[]{:S(2)}) %collective-permute-start.5) | collective-permute-done | bytes 2097184 | tf_op jit(solution)/shard_map/ppermute | solution.py:561
  894.7 40.5 %collective-permute-done.8 = bf16[512,2048]{1,0:T(8,128)(2,1)} collective-permute-done((bf16[512,2048]{1,0:T(8,128)(2,1)}, bf16[512,2048]{1,0:T(8,128)(2,1)}, u32[]{:S(2)}, u32[]{:S(2)}) %collective-permute-start.8) | collective-permute-done | bytes 2097184 | tf_op jit(solution)/shard_map/ppermute | solution.py:561
  938.2 86.8 %collective-permute-done.11 = bf16[512,2048]{1,0:T(8,128)(2,1)} collective-permute-done((bf16[512,2048]{1,0:T(8,128)(2,1)S(1)}, bf16[512,2048]{1,0:T(8,128)(2,1)}, u32[]{:S(2)}, u32[]{:S(2)}) %collective-permute-start.11) | collective-permute-done | bytes 2097184 | tf_op jit(solution)/shard_map/ppermute | solution.py:561
  1028.0 42.0 %collective-permute-done.17 = bf16[512,2048]{1,0:T(8,128)(2,1)} collective-permute-done((bf16[512,2048]{1,0:T(8,128)(2,1)}, bf16[512,2048]{1,0:T(8,128)(2,1)}, u32[]{:S(2)}, u32[]{:S(2)}) %collective-permute-start.17) | collective-permute-done | bytes 2097184 | tf_op jit(solution)/shard_map/ppermute | solution.py:561
  1074.8 34.9 %collective-permute-done.20 = bf16[512,2048]{1,0:T(8,128)(2,1)S(1)} collective-permute-done((bf16[512,2048]{1,0:T(8,128)(2,1)S(1)}, bf16[512,2048]{1,0:T(8,128)(2,1)S(1)}, u32[]{:S(2)}, u32[]{:S(2)}) %collective-permute-start.20) | collective-permute-done | bytes 2097184 | tf_op jit(solution)/shard_map/ppermute | solution.py:561
  (187 shorter events, 249.1 us)
Async XLA Ops:
  7.2 757.6 %reduce-scatter.7.cloned.1.call-start = ((), (), s32[]{:S(2)}) async-start(), calls=%async_computation.5 | async-start | bytes 2359296 | tf_op jit(solution)/shard_map/reduce_scatter | solution.py:639
  162.9 954.6 %reduce-scatter.5.cloned.1.call-start = ((), (), s32[]{:S(2)}) async-start(), calls=%async_computation.4 | async-start | bytes 7077888 | tf_op jit(solution)/shard_map/reduce_scatter | solution.py:639
  205.3 915.7 %reduce-scatter.9.cloned.1.call-start = ((), (), s32[]{:S(2)}) async-start(), calls=%async_computation.6 | async-start | bytes 9437184 | tf_op jit(solution)/shard_map/reduce_scatter | solution.py:639
  261.0 862.8 %reduce-scatter.11.cloned.1.call-start = ((), (), s32[]{:S(2)}) async-start(), calls=%async_computation.7 | async-start | bytes 9437184 | tf_op jit(solution)/shard_map/reduce_scatter | solution.py:639
  367.1 66.0 %collective-permute-start.21 = (bf16[512,2048]{1,0:T(8,128)(2,1)}, bf16[512,2048]{1,0:T(8,128)(2,1)}, u32[]{:S(2)}, u32[]{:S(2)}) collective-permute-start(bf16[512,2048]{1,0:T(8,128)(2,1)} %get-tuple-element.49), channel_id=1, source_target_pairs={{0,1},{3,2},{4,5},{7,6},{8,9},{11,10},{12,13},{15,14},{16,17},{19,... | collective-permute-start | bytes 6291464 | tf_op jit(solution)/shard_map/ppermute | solution.py:561
  369.7 89.9 %collective-permute-start.18 = (bf16[512,2048]{1,0:T(8,128)(2,1)}, bf16[512,2048]{1,0:T(8,128)(2,1)}, u32[]{:S(2)}, u32[]{:S(2)}) collective-permute-start(bf16[512,2048]{1,0:T(8,128)(2,1)} %get-tuple-element.48), channel_id=1, source_target_pairs={{0,1},{3,2},{4,5},{7,6},{8,9},{11,10},{12,13},{15,14},{16,17},{19,... | collective-permute-start | bytes 6291464 | tf_op jit(solution)/shard_map/ppermute | solution.py:561
  372.3 132.1 %collective-permute-start.15 = (bf16[512,2048]{1,0:T(8,128)(2,1)S(1)}, bf16[512,2048]{1,0:T(8,128)(2,1)}, u32[]{:S(2)}, u32[]{:S(2)}) collective-permute-start(bf16[512,2048]{1,0:T(8,128)(2,1)S(1)} %copy-done.8), channel_id=1, source_target_pairs={{0,1},{3,2},{4,5},{7,6},{8,9},{11,10},{12,13},{15,14},{16,17},{19,... | collective-permute-start | bytes 6291464 | tf_op jit(solution)/shard_map/ppermute | solution.py:561
  375.0 174.5 %collective-permute-start.12 = (bf16[512,2048]{1,0:T(8,128)(2,1)}, bf16[512,2048]{1,0:T(8,128)(2,1)}, u32[]{:S(2)}, u32[]{:S(2)}) collective-permute-start(bf16[512,2048]{1,0:T(8,128)(2,1)} %get-tuple-element.46), channel_id=1, source_target_pairs={{0,1},{3,2},{4,5},{7,6},{8,9},{11,10},{12,13},{15,14},{16,17},{19,... | collective-permute-start | bytes 6291464 | tf_op jit(solution)/shard_map/ppermute | solution.py:561
  427.3 167.2 %collective-permute-start.9 = (bf16[512,2048]{1,0:T(8,128)(2,1)}, bf16[512,2048]{1,0:T(8,128)(2,1)}, u32[]{:S(2)}, u32[]{:S(2)}) collective-permute-start(bf16[512,2048]{1,0:T(8,128)(2,1)} %branch_part.7), channel_id=1, source_target_pairs={{0,1},{3,2},{4,5},{7,6},{8,9},{11,10},{12,13},{15,14},{16,17},{19,... | collective-permute-start | bytes 6291464 | tf_op jit(solution)/shard_map/ppermute | solution.py:561
  433.1 206.3 %collective-permute-start = (bf16[512,2048]{1,0:T(8,128)(2,1)}, bf16[512,2048]{1,0:T(8,128)(2,1)}, u32[]{:S(2)}, u32[]{:S(2)}) collective-permute-start(bf16[512,2048]{1,0:T(8,128)(2,1)} %branch_part.4), channel_id=1, source_target_pairs={{0,1},{3,2},{4,5},{7,6},{8,9},{11,10},{12,13},{15,14},{16,17},{19,... | collective-permute-start | bytes 6291464 | tf_op jit(solution)/shard_map/ppermute | solution.py:561
  459.6 224.7 %collective-permute-start.3 = (bf16[512,2048]{1,0:T(8,128)(2,1)}, bf16[512,2048]{1,0:T(8,128)(2,1)}, u32[]{:S(2)}, u32[]{:S(2)}) collective-permute-start(bf16[512,2048]{1,0:T(8,128)(2,1)} %branch_part.5), channel_id=1, source_target_pairs={{0,1},{3,2},{4,5},{7,6},{8,9},{11,10},{12,13},{15,14},{16,17},{19,... | collective-permute-start | bytes 6291464 | tf_op jit(solution)/shard_map/ppermute | solution.py:561
  504.5 221.3 %collective-permute-start.6 = (bf16[512,2048]{1,0:T(8,128)(2,1)}, bf16[512,2048]{1,0:T(8,128)(2,1)S(1)}, u32[]{:S(2)}, u32[]{:S(2)}) collective-permute-start(bf16[512,2048]{1,0:T(8,128)(2,1)} %branch_part.6), channel_id=1, source_target_pairs={{0,1},{3,2},{4,5},{7,6},{8,9},{11,10},{12,13},{15,14},{16,17},{19,... | collective-permute-start | bytes 6291464 | tf_op jit(solution)/shard_map/ppermute | solution.py:561
  549.5 179.2 %collective-permute-start.22 = (bf16[512,2048]{1,0:T(8,128)(2,1)S(1)}, bf16[512,2048]{1,0:T(8,128)(2,1)S(1)}, u32[]{:S(2)}, u32[]{:S(2)}) collective-permute-start(bf16[512,2048]{1,0:T(8,128)(2,1)S(1)} %add.181), channel_id=1, source_target_pairs={{1,2},{2,1},{5,6},{6,5},{9,10},{10,9},{13,14},{14,13},{17,18},{18,... | collective-permute-start | bytes 6291464 | tf_op jit(solution)/shard_map/ppermute | solution.py:561
  594.5 140.0 %collective-permute-start.19 = (bf16[512,2048]{1,0:T(8,128)(2,1)S(1)}, bf16[512,2048]{1,0:T(8,128)(2,1)S(1)}, u32[]{:S(2)}, u32[]{:S(2)}) collective-permute-start(bf16[512,2048]{1,0:T(8,128)(2,1)S(1)} %add.178), channel_id=1, source_target_pairs={{1,2},{2,1},{5,6},{6,5},{9,10},{10,9},{13,14},{14,13},{17,18},{18,... | collective-permute-start | bytes 6291464 | tf_op jit(solution)/shard_map/ppermute | solution.py:561
  639.4 101.6 %collective-permute-start.13 = (bf16[512,2048]{1,0:T(8,128)(2,1)S(1)}, bf16[512,2048]{1,0:T(8,128)(2,1)S(1)}, u32[]{:S(2)}, u32[]{:S(2)}) collective-permute-start(bf16[512,2048]{1,0:T(8,128)(2,1)S(1)} %add.172), channel_id=1, source_target_pairs={{1,2},{2,1},{5,6},{6,5},{9,10},{10,9},{13,14},{14,13},{17,18},{18,... | collective-permute-start | bytes 6291464 | tf_op jit(solution)/shard_map/ppermute | solution.py:561
  684.4 60.8 %collective-permute-start.1 = (bf16[512,2048]{1,0:T(8,128)(2,1)S(1)}, bf16[512,2048]{1,0:T(8,128)(2,1)S(1)}, u32[]{:S(2)}, u32[]{:S(2)}) collective-permute-start(bf16[512,2048]{1,0:T(8,128)(2,1)S(1)} %add.150), channel_id=1, source_target_pairs={{1,2},{2,1},{5,6},{6,5},{9,10},{10,9},{13,14},{14,13},{17,18},{18,... | collective-permute-start | bytes 6291464 | tf_op jit(solution)/shard_map/ppermute | solution.py:561
  745.2 55.2 %collective-permute-start.14 = (bf16[512,2048]{1,0:T(8,128)(2,1)}, bf16[512,2048]{1,0:T(8,128)(2,1)}, u32[]{:S(2)}, u32[]{:S(2)}) collective-permute-start(bf16[512,2048]{1,0:T(8,128)(2,1)} %add.173), channel_id=1, source_target_pairs={{1,0},{2,3},{5,4},{6,7},{9,8},{10,11},{13,12},{14,15},{17,16},{18,... | collective-permute-start | bytes 6291464 | tf_op jit(solution)/shard_map/ppermute | solution.py:561
  750.1 95.2 %collective-permute-start.2 = (bf16[512,2048]{1,0:T(8,128)(2,1)}, bf16[512,2048]{1,0:T(8,128)(2,1)}, u32[]{:S(2)}, u32[]{:S(2)}) collective-permute-start(bf16[512,2048]{1,0:T(8,128)(2,1)} %add.151), channel_id=1, source_target_pairs={{1,0},{2,3},{5,4},{6,7},{9,8},{10,11},{13,12},{14,15},{17,16},{18,... | collective-permute-start | bytes 6291464 | tf_op jit(solution)/shard_map/ppermute | solution.py:561
  755.9 134.4 %collective-permute-start.5 = (bf16[512,2048]{1,0:T(8,128)(2,1)}, bf16[512,2048]{1,0:T(8,128)(2,1)}, u32[]{:S(2)}, u32[]{:S(2)}) collective-permute-start(bf16[512,2048]{1,0:T(8,128)(2,1)} %add.158), channel_id=1, source_target_pairs={{1,0},{2,3},{5,4},{6,7},{9,8},{10,11},{13,12},{14,15},{17,16},{18,... | collective-permute-start | bytes 6291464 | tf_op jit(solution)/shard_map/ppermute | solution.py:561
  762.9 172.3 %collective-permute-start.8 = (bf16[512,2048]{1,0:T(8,128)(2,1)}, bf16[512,2048]{1,0:T(8,128)(2,1)}, u32[]{:S(2)}, u32[]{:S(2)}) collective-permute-start(bf16[512,2048]{1,0:T(8,128)(2,1)} %add.162), channel_id=1, source_target_pairs={{1,0},{2,3},{5,4},{6,7},{9,8},{10,11},{13,12},{14,15},{17,16},{18,... | collective-permute-start | bytes 6291464 | tf_op jit(solution)/shard_map/ppermute | solution.py:561
  775.8 337.0 %collective-permute-start.23 = (bf16[512,2048]{1,0:T(8,128)(2,1)}, bf16[512,2048]{1,0:T(8,128)(2,1)}, u32[]{:S(2)}, u32[]{:S(2)}) collective-permute-start(bf16[512,2048]{1,0:T(8,128)(2,1)} %add.182), channel_id=1, source_target_pairs={{1,0},{2,3},{5,4},{6,7},{9,8},{10,11},{13,12},{14,15},{17,16},{18,... | collective-permute-start | bytes 6291464 | tf_op jit(solution)/shard_map/ppermute | solution.py:561
  800.4 224.7 %collective-permute-start.11 = (bf16[512,2048]{1,0:T(8,128)(2,1)S(1)}, bf16[512,2048]{1,0:T(8,128)(2,1)}, u32[]{:S(2)}, u32[]{:S(2)}) collective-permute-start(bf16[512,2048]{1,0:T(8,128)(2,1)S(1)} %add.166), channel_id=1, source_target_pairs={{1,0},{2,3},{5,4},{6,7},{9,8},{10,11},{13,12},{14,15},{17,16},{18,... | collective-permute-start | bytes 6291464 | tf_op jit(solution)/shard_map/ppermute | solution.py:561
  845.3 224.7 %collective-permute-start.17 = (bf16[512,2048]{1,0:T(8,128)(2,1)}, bf16[512,2048]{1,0:T(8,128)(2,1)}, u32[]{:S(2)}, u32[]{:S(2)}) collective-permute-start(bf16[512,2048]{1,0:T(8,128)(2,1)} %add.176), channel_id=1, source_target_pairs={{1,0},{2,3},{5,4},{6,7},{9,8},{10,11},{13,12},{14,15},{17,16},{18,... | collective-permute-start | bytes 6291464 | tf_op jit(solution)/shard_map/ppermute | solution.py:561
  890.3 219.4 %collective-permute-start.20 = (bf16[512,2048]{1,0:T(8,128)(2,1)S(1)}, bf16[512,2048]{1,0:T(8,128)(2,1)S(1)}, u32[]{:S(2)}, u32[]{:S(2)}) collective-permute-start(bf16[512,2048]{1,0:T(8,128)(2,1)S(1)} %add.179), channel_id=1, source_target_pairs={{1,0},{2,3},{5,4},{6,7},{9,8},{10,11},{13,12},{14,15},{17,16},{18,... | collective-permute-start | bytes 6291464 | tf_op jit(solution)/shard_map/ppermute | solution.py:561
  (32 other events, 1682.6 us)
Sparse Core Ops, SparseCore 0:
  163.1 41.8 reduce-scatter.6
  208.3 61.7 reduce-scatter.4
  273.5 71.4 reduce-scatter.8
  401.9 70.1 reduce-scatter.10
